TPU v7x, 32 devices: a whole 2x2x4 slice. The times are simulated.
32 devices in a mesh: rep: 2 (over y), tile: 4 (over z), pen: 2 (over x), sub: 2 (over core).
Axes of the slice: x: 2, y: 2, z: 4, core: 2. Of those that a mesh axis runs over, the one named last changes fastest.
Arguments:
- positions: float32 [6, 4, 2, 512], P('rep', 'tile', 'pen'), parts along dimension 0, may hold values from 0 to 256, as said below
- velocities: float32 [6, 4, 2, 512], P('rep', 'tile', 'pen'), parts along dimension 0, may hold values from -5 to 5
- charges: float32 [8, 2, 512], P(('rep', 'tile'), 'pen'), parts along dimension 0, may hold values from -3 to 3
- inverse_mass: float32 [8, 2, 512], P(('rep', 'tile'), 'pen'), parts along dimension 0, may hold values from 0.06 to 1
- export_rows: int32 [8, 2, 128], P(('rep', 'tile'), 'pen'), parts along dimension 0, may hold values from 0 to 511, as said below
- partners: int32 [8, 2, 64, 512], P(('rep', 'tile'), 'pen', 'sub'), parts along dimension 0, may hold values from 0 to 1663, as said below
- bond_partners: int32 [8, 2, 4, 512], P(('rep', 'tile'), 'pen', 'sub'), parts along dimension 0, may hold values from 0 to 511, as said below
- bond_rest: float32 [8, 2, 4, 512], P(('rep', 'tile'), 'pen', 'sub'), parts along dimension 0, may hold values from 1 to 8
- block_offsets: int32 [6, 4, 2, 512], P('rep', 'tile', 'pen'), parts along dimension 0, may hold values from -1 to 254, as said below
Outputs:
- final_positions: float32 [6, 4, 2, 512], P('rep', 'tile', 'pen'), parts along dimension 0
- final_velocities: float32 [6, 4, 2, 512], P('rep', 'tile', 'pen'), parts along dimension 0
- potential: float32 [8, 2, 512], P(('rep', 'tile'), 'pen', 'sub'), parts along dimension 0
There are 2 independent parts, one for each index of `rep`. A program takes and returns all parts, laid end to end along the dimension named above; each array names one. Nothing has to cross between parts.
Inputs may be any that keep to these rules, and one draw needn't show every extreme that they name: `positions`: coordinates of an atom lie strictly between its block offset + 1 and its block offset + 2, coordinate by coordinate. `block_offsets`: for the patch (t, p), x offsets lie in t * 64 - 1 to t * 64 + 62 and y offsets in p * 128 - 1 to p * 128 + 126; z offsets lie in -1 to 254. `export_rows`: rows of the patch's own atoms. `partners`: columns of the patch's table; columns 1024 to 1151 are never named. Slots that an atom does not use name the atom itself. `bond_partners`: rows of the patch's own atoms.
All inputs are finite; a program needn't handle non-finite values.
Results may differ from a plain program's by a relative error of at most 0.0005.
Values sent between devices are 32-bit elements; how exact they have to be, the bound alone decides.
A program may use at most 128 MiB of HBM per device.

v0:
```python
import functools
import math

import jax
import jax.numpy as jnp
import numpy as np
from jax import lax
from jax.experimental import pallas as pl
from jax.experimental.pallas import tpu as pltpu
from jax.sharding import PartitionSpec as P

GRID = 256
INNER = 4
LANES = 128

time_step = 0.1
coulomb = 30.0
bond_stiffness = 0.2
soften = 1.0
cutoff_sq = 144.0
ewald_beta = 0.32

f32 = jnp.float32
bf16 = jnp.bfloat16


def lane_gather(rows, low):
    return jnp.take_along_axis(rows, low, axis=1, mode="promise_in_bounds")


def shown_rows(state, shown):
    index = jnp.broadcast_to(shown, (8, shown.shape[1]))
    low, high = index & (LANES - 1), index >> 7
    total = jnp.zeros((8, shown.shape[1]), f32)
    for block in range(state.shape[1] // LANES):
        part = lane_gather(state[:, block * LANES : (block + 1) * LANES], low)
        total = jnp.where(high == block, part, total)
    return total[:4]


def dynamics_kernel(
    state_ref, shown_ref, partners_ref, bonds_ref, rest_ref,
    out_ref, table, sent, beside, send_sem, recv_sem, *, tile_count, pen_count,
):
    tile_index, pen_index = lax.axis_index("tile"), lax.axis_index("pen")
    around = [(i, j) for i in range(3) for j in range(3) if (i, j) != (1, 1)]

    def neighbour(i, j):
        return {
            "tile": lax.rem(tile_index + (i - 1) + tile_count, tile_count),
            "pen": lax.rem(pen_index + (j - 1) + pen_count, pen_count),
        }

    barrier = pltpu.get_barrier_semaphore()
    for i, j in around:
        pl.semaphore_signal(
            barrier, inc=1, device_id=neighbour(i, j), device_id_type=pl.DeviceIdType.MESH
        )
    pl.semaphore_wait(barrier, len(around))
    out_ref[...] = state_ref[...]

    def step(n, carry):
        sent[n] = shown_rows(out_ref[...], shown_ref[...])
        copies = []
        for place, (i, j) in enumerate(around):
            copy = pltpu.make_async_remote_copy(
                src_ref=sent.at[n],
                dst_ref=beside.at[n, len(around) - 1 - place],
                send_sem=send_sem.at[n, place],
                recv_sem=recv_sem.at[n, len(around) - 1 - place],
                device_id=neighbour(i, j),
                device_id_type=pl.DeviceIdType.MESH,
            )
            copy.start()
            copies.append(copy)
        one_step(
            tile_index, pen_index, tile_count, pen_count, n, copies, around,
            out_ref, beside, partners_ref, bonds_ref, rest_ref, table,
        )
        return carry

    lax.fori_loop(0, INNER, step, 0)


def one_step(
    tile_index, pen_index, tile_count, pen_count, n, copies, around,
    state_ref, beside_ref, partners_ref, bonds_ref, rest_ref, table,
):
    out_ref = state_ref
    atoms = state_ref.shape[1]
    own_blocks = atoms // LANES
    halo_blocks = beside_ref.shape[3] // LANES
    blocks = list(range(own_blocks))
    for block in range(own_blocks):
        for row in range(4):
            table[block * 4 + row] = jnp.broadcast_to(
                state_ref[row : row + 1, block * LANES : (block + 1) * LANES], (8, LANES)
            )
    for copy in copies:
        copy.wait()
    for i in range(3):
        near_x = tile_index + (i - 1)
        move_x = jnp.where(near_x < 0, -float(GRID), jnp.where(near_x >= tile_count, float(GRID), 0.0))
        for j in range(3):
            if i == 1 and j == 1:
                continue
            near_y = pen_index + (j - 1)
            move_y = jnp.where(near_y < 0, -float(GRID), jnp.where(near_y >= pen_count, float(GRID), 0.0))
            patch = beside_ref[n, around.index((i, j))]
            for part in range(halo_blocks):
                block = own_blocks + (i * 3 + j) * halo_blocks + part
                blocks.append(block)
                for row in range(4):
                    line = patch[row : row + 1, part * LANES : (part + 1) * LANES]
                    if row == 0:
                        line = line + move_x
                    if row == 1:
                        line = line + move_y
                    table[block * 4 + row] = jnp.broadcast_to(line, (8, LANES))

    def fetch(index, rows, among):
        low, high = index & (LANES - 1), index >> 7
        found = [jnp.zeros((8, LANES), f32) for _ in range(rows)]
        for block in among:
            hit = high == block
            for row in range(rows):
                found[row] = jnp.where(hit, lane_gather(table[block * 4 + row], low), found[row])
        return found

    for c in range(own_blocks):
        lanes = slice(c * LANES, (c + 1) * LANES)
        own = [jnp.broadcast_to(state_ref[r : r + 1, lanes], (8, LANES)) for r in range(4)]

        def slots(g, force, lanes=lanes, own=own):
            index = partners_ref[pl.ds(pl.multiple_of(g * 8, 8), 8), lanes]
            near = fetch(index, 4, blocks)
            delta = [own[r] - near[r] for r in range(3)]
            dist_sq = delta[0] * delta[0] + delta[1] * delta[1] + delta[2] * delta[2]
            taper = 1.0 - dist_sq / cutoff_sq
            taper = jnp.where(dist_sq < cutoff_sq, taper * taper, 0.0)
            root = lax.rsqrt(dist_sq + soften)
            strength = coulomb * own[3] * near[3] * taper * (root * root * root)
            return tuple(force[r] + strength * delta[r] for r in range(3))

        def bonded(g, force, lanes=lanes, own=own):
            rows = pl.ds(pl.multiple_of(g * 8, 8), 8)
            near = fetch(bonds_ref[rows, lanes], 3, range(own_blocks))
            delta = [own[r] - near[r] for r in range(3)]
            root = lax.rsqrt(delta[0] * delta[0] + delta[1] * delta[1] + delta[2] * delta[2] + soften)
            pull = -bond_stiffness * (1.0 - rest_ref[rows, lanes] * root)
            return tuple(force[r] + pull * delta[r] for r in range(3))

        force = tuple(jnp.zeros((8, LANES), f32) for _ in range(3))
        force = lax.fori_loop(0, partners_ref.shape[0] // 8, slots, force)
        force = lax.fori_loop(0, bonds_ref.shape[0] // 8, bonded, force)
        scale = state_ref[7:8, lanes]
        for r in range(3):
            total = jnp.sum(force[r], axis=0, keepdims=True)
            speed = state_ref[4 + r : 5 + r, lanes] + time_step * scale * total
            out_ref[4 + r : 5 + r, lanes] = speed
            out_ref[r : r + 1, lanes] = state_ref[r : r + 1, lanes] + time_step * speed
        out_ref[3:4, lanes] = state_ref[3:4, lanes]
        out_ref[7:8, lanes] = scale


def split(value):
    high = value.astype(bf16)
    return high, (value - high.astype(f32)).astype(bf16)


def product(left, right, turned=False):
    dims = (((1,), (1 if turned else 0,)), ((), ()))

    def dot(a, b):
        return lax.dot_general(a, b, dims, preferred_element_type=f32)

    return dot(left[0], right[0]) + (dot(left[0], right[1]) + dot(left[1], right[0]))


def spline(place, frac):
    rest = 1.0 - frac
    square = frac * frac
    cube = square * frac
    pieces = (
        rest * rest * rest / 6.0,
        (3.0 * cube - 6.0 * square + 4.0) / 6.0,
        (-3.0 * cube + 3.0 * square + 3.0 * frac + 1.0) / 6.0,
        cube / 6.0,
    )
    total = jnp.zeros(place.shape, f32)
    for order in range(4):
        total = jnp.where(place == order, pieces[order], total)
    return total


def mesh_kernel(
    first_ref, lines_ref, squares_ref, atoms_ref, mine_ref, cas_ref, wide_ref, tall_ref, along_ref, across_ref,
    out_ref, grid, wx, wy, wz, *, planes, chunk, keep,
):
    tiles, share, deep = grid.shape[0], grid.shape[1], grid.shape[2]
    atoms = atoms_ref.shape[2]
    first = first_ref[0]

    def cells(offset, count):
        return lax.broadcasted_iota(jnp.int32, (count, atoms), 0) - offset

    def prepare(s):
        own = atoms_ref[s]
        offset = own[3:6].astype(jnp.int32)
        depth = spline(cells(offset[2:3], GRID) & (GRID - 1), own[2:3])
        return product((cas_ref[0], cas_ref[1]), split(depth))

    def tile_of(s):
        apart = first_ref[1] - s
        return jnp.where(apart < 0, apart + tiles, apart)

    def spread(s, carry):
        t = tile_of(s)
        own = atoms_ref[s]
        offset = own[3:6].astype(jnp.int32)
        wx[t] = spline(cells(offset[0:1] - (t * planes - 1), deep), own[0:1])
        rows = spline(cells(offset[1:2], GRID) & (GRID - 1), own[1:2])
        wy[t] = product((mine_ref[0], mine_ref[1]), split(rows))
        depth = prepare(s)
        if keep:
            high, low = split(depth)
            wz[t, 0] = high
            wz[t, 1] = low
        charged = split(depth * own[6:7])
        for c in range(0, share, chunk):
            pieces = [wx[t] * wy[t, k : k + 1, :] for k in range(c, c + chunk)]
            plane = split(jnp.concatenate(pieces, axis=0))
            grid[t, c : c + chunk] = product(plane, charged, True).reshape(chunk, deep, GRID)
        return carry

    lax.fori_loop(0, tiles, spread, 0)

    def transform(k, carry):
        line = grid[:, k].reshape(tiles * deep, GRID)
        spectrum = product((wide_ref[0], wide_ref[1]), split(line))
        m_sq = along_ref[...] + squares_ref[first + k]
        anchor = m_sq == 0.0
        value = across_ref[...] * lines_ref[first + k] / jnp.where(anchor, 1.0, m_sq)
        weighted = spectrum * jnp.where(anchor, 0.0, value)
        back = product((tall_ref[0], tall_ref[1]), split(weighted))
        grid[:, k] = back.reshape(tiles, deep, GRID)
        return carry

    lax.fori_loop(0, share, transform, 0)

    def read(s, carry):
        t = tile_of(s)
        if keep:
            depth = (wz[t, 0], wz[t, 1])
        else:
            depth = split(prepare(s))
        total = jnp.zeros((deep, atoms), f32)
        for c in range(0, share, chunk):
            line = split(grid[t, c : c + chunk].reshape(chunk * deep, GRID))
            values = product(line, depth)
            for k in range(chunk):
                total = total + values[k * deep : (k + 1) * deep] * wy[t, c + k : c + k + 1, :]
        out_ref[s] = jnp.sum(total * wx[t], axis=0, keepdims=True)
        return carry

    lax.fori_loop(0, tiles, read, 0)


def halves(table):
    table = jnp.asarray(table.astype(np.float32))
    return jnp.stack(split(table))


def tables(tiles, planes, deep):
    index = np.arange(GRID)
    angle = 2.0 * math.pi / GRID * np.mod(index[:, None] * index[None, :], GRID)
    cas = np.cos(angle) + np.sin(angle)
    place = np.mod(np.arange(tiles)[:, None] * planes - 1 + np.arange(deep)[None, :], GRID).reshape(-1)
    wide = cas[:, place]
    signed = np.where(index > GRID // 2, index - GRID, index).astype(np.float64)
    turn = 2.0 * math.pi / GRID * index
    real = (1.0 + 4.0 * np.cos(turn) + np.cos(2.0 * turn)) / 6.0
    imag = (4.0 * np.sin(turn) + np.sin(2.0 * turn)) / 6.0
    square = signed**2 / float(GRID * GRID)
    line = np.exp(-((math.pi / ewald_beta) ** 2) * square) / (real * real + imag * imag)
    along = square[:, None] + square[None, :]
    across = line[:, None] * line[None, :] / (math.pi * float(GRID) ** 3)
    return cas, wide, line.astype(np.float32), square.astype(np.float32), along.astype(np.float32), across.astype(np.float32)


def passed_along(value, axis, steps):
    count = lax.axis_size(axis)
    pairs = [(source, (source + steps) % count) for source in range(count)]
    return lax.ppermute(value, axis, pairs)


def on_device(
    positions, velocities, charges, inverse_mass, export_rows, partners, bond_partners, bond_rest, block_offsets,
):
    tile_count = lax.axis_size("tile")
    pen_count = lax.axis_size("pen")
    half_count = lax.axis_size("sub")
    patches = tile_count * pen_count
    tile_index = lax.axis_index("tile")
    pen_index = lax.axis_index("pen")
    atoms = positions.shape[3]
    exported = export_rows.shape[2]
    planes = GRID // tile_count
    state = jnp.concatenate(
        [positions[:, 0, 0], charges[0], velocities[:, 0, 0], inverse_mass[0]], axis=0
    )
    shown = export_rows[0]
    neighbours = lax.all_gather(
        jnp.concatenate([partners[0, 0], bond_partners[0, 0]], axis=0), "sub", axis=0
    )
    rest = lax.all_gather(bond_rest[0, 0], "sub", axis=0, tiled=True)
    slots = partners.shape[2]
    near = neighbours[:, :slots].reshape(-1, atoms)
    bonds = neighbours[:, slots:].reshape(-1, atoms)
    fill = -bonds.shape[0] % 8
    self_rows = jnp.broadcast_to(jnp.arange(atoms, dtype=jnp.int32), (fill, atoms))
    bonds = jnp.concatenate([bonds, self_rows], axis=0)
    rest = jnp.concatenate([rest, jnp.ones((fill, atoms), f32)], axis=0)
    vmem = pl.BlockSpec(memory_space=pltpu.VMEM)
    smem = pl.BlockSpec(memory_space=pltpu.SMEM)
    columns = (atoms + 9 * exported) // LANES
    state = pl.pallas_call(
        functools.partial(dynamics_kernel, tile_count=tile_count, pen_count=pen_count),
        out_shape=jax.ShapeDtypeStruct(state.shape, f32),
        in_specs=[vmem] * 5,
        out_specs=vmem,
        scratch_shapes=[
            pltpu.VMEM((columns * 4, 8, LANES), f32),
            pltpu.VMEM((INNER, 4, exported), f32),
            pltpu.VMEM((INNER, 8, 4, exported), f32),
            pltpu.SemaphoreType.DMA((INNER, 8)),
            pltpu.SemaphoreType.DMA((INNER, 8)),
        ],
        compiler_params=pltpu.CompilerParams(collective_id=0, has_side_effects=True),
    )(state, shown, near, bonds, rest)
    coords, speeds = state[0:3], state[4:7]
    offsets = block_offsets[:, 0, 0].astype(f32)
    packed = jnp.concatenate([coords - (offsets + 1.0), offsets, state[3:4], state[3:4]], axis=0)
    row = jnp.concatenate(
        [packed] + [passed_along(packed, "pen", step) for step in range(1, pen_count)], axis=1
    )
    every = jnp.stack([row] + [passed_along(row, "tile", step) for step in range(1, tile_count)])
    share = GRID // (patches * half_count)
    chunk = math.gcd(share, 8)
    unit = 8 if chunk % 2 == 0 else 16
    deep = -(-(planes + 3) // unit) * unit
    wide_atoms = pen_count * atoms
    keep = patches * atoms * GRID * 4 <= 8 * 1024 * 1024
    cas, wide, line, square, along, across = tables(tile_count, planes, deep)
    start = (lax.axis_index(("tile", "pen", "sub")) * share).astype(jnp.int32)
    first = jnp.stack([start, tile_index.astype(jnp.int32)])
    partial_value = pl.pallas_call(
        functools.partial(mesh_kernel, planes=planes, chunk=chunk, keep=keep),
        out_shape=jax.ShapeDtypeStruct((tile_count, 1, wide_atoms), f32),
        in_specs=[smem] * 3 + [vmem] * 7,
        out_specs=vmem,
        scratch_shapes=[
            pltpu.VMEM((tile_count, share, deep, GRID), f32),
            pltpu.VMEM((tile_count, deep, wide_atoms), f32),
            pltpu.VMEM((tile_count, share, wide_atoms), f32),
            pltpu.VMEM((tile_count if keep else 1, 2, GRID, wide_atoms), bf16),
        ],
        compiler_params=pltpu.CompilerParams(vmem_limit_bytes=60 * 1024 * 1024),
    )(
        first, jnp.asarray(line), jnp.asarray(square), every,
        lax.dynamic_slice_in_dim(halves(cas), start, share, axis=1), halves(cas), halves(wide), halves(wide.T), jnp.asarray(along), jnp.asarray(across),
    )
    sums = partial_value[0]
    for step in range(1, tile_count):
        sums = sums + passed_along(partial_value[step], "tile", -step)
    own = sums[:, :atoms]
    for step in range(1, pen_count):
        own = own + passed_along(sums[:, step * atoms : (step + 1) * atoms], "pen", -step)
    half = lax.axis_index("sub")
    width = atoms // half_count
    potential = lax.dynamic_slice_in_dim(own, half * width, width, 1)
    for step in range(1, half_count):
        other = (half + step) % half_count
        potential = potential + passed_along(
            lax.dynamic_slice_in_dim(own, other * width, width, 1), "sub", step
        )
    potential = potential.reshape(-1)
    return (coords[:, None, None, :], speeds[:, None, None, :], potential[None, None, :])


def solution(mesh):
    placed = (
        P("rep", "tile", "pen", None),
        P("rep", "tile", "pen", None),
        P(("rep", "tile"), "pen", None),
        P(("rep", "tile"), "pen", None),
        P(("rep", "tile"), "pen", None),
        P(("rep", "tile"), "pen", "sub", None),
        P(("rep", "tile"), "pen", "sub", None),
        P(("rep", "tile"), "pen", "sub", None),
        P("rep", "tile", "pen", None),
    )
    return jax.shard_map(
        on_device,
        mesh=mesh,
        in_specs=placed,
        out_specs=(
            P("rep", "tile", "pen", None),
            P("rep", "tile", "pen", None),
            P(("rep", "tile"), "pen", "sub"),
        ),
        check_vma=False,
    )
```

profile of v0, /device:TPU:0, one launch (start us, length us, event | category | flops | bytes accessed | tf_op | source)
XLA Modules:
  0.0 118.1 jit_solution(5910718495609777927)
XLA Ops:
  0.6 0.9 add_bitcast_fusion
  1.5 2.0 %all-gather.2 = s32[2,34,512]{2,1,0:T(8,128)S(1)} all-gather(s32[1,34,512]{2,1,0:T(8,128)S(1)} %add_bitcast_fusion), channel_id=2, replica_groups=mesh['rep'=2,'tile'=4,'pen'=2,'sub'=2] {'sub'}, dimensions={0}, use_global_device_ids=true | all-gather | bytes 208896 | tf_op jit(solution)/shard_map/all_gather | solution.py:313
  3.5 0.7 slice.45
  4.2 0.0 copy-start.3
  4.2 0.7 copy-done.3
  4.9 1.8 %all-gather.1 = f32[1,1,4,512]{3,1,0,2:T(1,128)S(1)} all-gather(f32[1,1,2,512]{3,1,0,2:T(1,128)S(1)} %copy.23), channel_id=3, replica_groups=mesh['rep'=2,'tile'=4,'pen'=2,'sub'=2] {'sub'}, dimensions={2}, use_global_device_ids=true | all-gather | bytes 12288 | tf_op jit(solution)/shard_map/all_gather | solution.py:316
  6.7 0.0 copy-start.1
  6.7 0.0 copy-start.2
  6.7 0.7 copy-done.1
  7.4 0.0 copy-done.2
  7.4 0.6 pad_add_fusion.bonds_ref
  8.0 0.6 concatenate.21.rest_ref
  8.6 0.0 copy-start.5
  8.6 0.0 copy-start.4
  8.6 0.7 copy-done.5
  9.3 0.0 copy-done.4
  9.3 0.6 pad_maximum_fusion.2.state_ref
  10.0 43.4 %shard_map.184 = f32[8,512]{1,0:T(8,128)} custom-call(f32[8,512]{1,0:T(8,128)} %pad_maximum_fusion.2.state_ref, s32[1,128]{1,0:T(1,128)} %bitcast.55, s32[64,512]{1,0:T(8,128)} %bitcast.45, s32[8,512]{1,0:T(8,128)} %pad_add_fusion.bonds_ref, f32[8,512]{1,0:T(8,128)} %concatenate.21.rest_ref), custom_call_target="tpu_custom_call" | custom-call | tf_op jit(solution)/shard_map/pallas_call | solution.py:327
  53.3 0.7 slice.38
  54.1 0.0 copy-done
  54.1 0.8 add_subtract_fusion
  54.9 0.6 collective-permute-start
  55.5 1.3 %constant_dynamic-slice_fusion.1.mine_ref = bf16[2,16,256]{2,1,0:T(8,128)(2,1)} fusion(bf16[2,256,256]{2,1,0:T(8,128)(2,1)} %constant.75.cas_ref, s32[]{:T(128)S(6)} %select_n.16), kind=kLoop, calls=%fused_computation.24 | loop fusion | bytes 32772 | tf_op jit(solution)/shard_map/dynamic_slice | solution.py:371
  56.8 1.9 %collective-permute-done = f32[8,512]{1,0:T(8,128)S(1)} collective-permute-done((f32[8,512]{1,0:T(8,128)S(1)}, f32[8,512]{1,0:T(8,128)S(1)}, u32[]{:S(2)}, u32[]{:S(2)}) %collective-permute-start) | collective-permute-done | bytes 16416 | tf_op jit(solution)/shard_map/ppermute | solution.py:294
  58.7 0.1 collective-permute-start.1
  58.8 1.2 %collective-permute-start.2 = (f32[8,1024]{1,0:T(8,128)S(1)}, f32[8,1024]{1,0:T(8,128)S(1)}, u32[]{:S(2)}, u32[]{:S(2)}) collective-permute-start(f32[8,1024]{1,0:T(8,128)S(1)} %pad_maximum_fusion.1), channel_id=1, source_target_pairs={{0,8},{4,12},{8,0},{12,4},{1,9},{5,13},{9,1},{13,5},{2,10},{6,14},... | collective-permute-start | bytes 98312 | tf_op jit(solution)/shard_map/ppermute | solution.py:294
  60.0 2.6 %collective-permute-start.3 = (f32[8,1024]{1,0:T(8,128)S(1)}, f32[8,1024]{1,0:T(8,128)S(1)}, u32[]{:S(2)}, u32[]{:S(2)}) collective-permute-start(f32[8,1024]{1,0:T(8,128)S(1)} %pad_maximum_fusion.1), channel_id=1, source_target_pairs={{0,12},{4,0},{8,4},{12,8},{1,13},{5,1},{9,5},{13,9},{2,14},{6,2},{... | collective-permute-start | bytes 98312 | tf_op jit(solution)/shard_map/ppermute | solution.py:294
  62.6 0.6 pad_add_fusion.1.first_ref
  63.2 1.3 %collective-permute-done.1 = f32[8,1024]{1,0:T(8,128)S(1)} collective-permute-done((f32[8,1024]{1,0:T(8,128)S(1)}, f32[8,1024]{1,0:T(8,128)S(1)}, u32[]{:S(2)}, u32[]{:S(2)}) %collective-permute-start.1) | collective-permute-done | bytes 32800 | tf_op jit(solution)/shard_map/ppermute | solution.py:294
  64.5 0.0 collective-permute-done.2
  64.5 0.6 collective-permute-done.3
  65.0 0.7 pad_maximum_fusion.atoms_ref
  65.7 36.7 %shard_map.185 = f32[4,1,1024]{2,1,0:T(1,128)} custom-call(s32[2]{0:T(128)} %pad_add_fusion.1.first_ref, f32[256]{0:T(256)} %constant.51.clone.lines_ref, f32[256]{0:T(256)} %constant.52.clone.squares_ref, f32[4,8,1024]{2,1,0:T(8,128)} %pad_maximum_fusion.atoms_ref, bf16[2,16,256]{2,1,0:T(8,128)(2,1)} %constant_dynamic-slice_fusion.1.mine_ref, ...), custom_call_target="tpu_custom_call" | custom-call | tf_op jit(solution)/shard_map/pallas_call | solution.py:357
  102.4 0.7 slice_bitcast_fusion.4
  103.1 3.3 %collective-permute-start.4 = (f32[1,1024]{1,0:T(1,128)S(1)}, f32[1,1024]{1,0:T(1,128)S(1)}, u32[]{:S(2)}, u32[]{:S(2)}) collective-permute-start(f32[1,1024]{1,0:T(1,128)S(1)} %get-tuple-element.9), channel_id=1, source_target_pairs={{0,12},{4,0},{8,4},{12,8},{1,13},{5,1},{9,5},{13,9},{2,14},{6,2},{... | collective-permute-start | bytes 12296 | tf_op jit(solution)/shard_map/ppermute | solution.py:294
  106.3 0.2 collective-permute-start.5
  106.6 0.3 collective-permute-start.6
  106.9 0.8 collective-permute-done.4
  107.7 3.2 %collective-permute-done.5 = f32[1,1024]{1,0:T(1,128)S(1)} collective-permute-done((f32[1,1024]{1,0:T(1,128)S(1)}, f32[1,1024]{1,0:T(1,128)S(1)}, u32[]{:S(2)}, u32[]{:S(2)}) %collective-permute-start.5) | collective-permute-done | bytes 4128 | tf_op jit(solution)/shard_map/ppermute | solution.py:294
  110.8 1.1 collective-permute-done.6
  112.0 0.7 fusion.3
  112.7 0.6 collective-permute-start.7
  113.3 3.0 %collective-permute-done.7 = f32[1,512]{1,0:T(1,128)S(1)} collective-permute-done((f32[1,512]{1,0:T(1,128)S(1)}, f32[1,512]{1,0:T(1,128)S(1)}, u32[]{:S(2)}, u32[]{:S(2)}) %collective-permute-start.7) | collective-permute-done | bytes 2080 | tf_op jit(solution)/shard_map/ppermute | solution.py:294
  116.3 0.0 collective-permute-start.8
  116.3 0.6 copy.25
  116.9 0.6 copy.26
  117.5 0.0 collective-permute-done.8
  117.5 0.6 add_bitcast_fusion.1
  (13 shorter events, 0.1 us)
Async XLA Ops:
  4.2 0.7 copy-start.3
  6.7 0.7 copy-start.1
  6.7 0.7 copy-start.2
  8.6 0.7 copy-start.5
  8.6 0.7 copy-start.4
  10.0 44.1 %copy-start = (s32[3,1,1,512]{3,2,1,0:T(1,128)S(1)}, s32[3,1,1,512]{3,2,1,0:T(1,128)}, u32[]{:S(2)}) copy-start(s32[3,1,1,512]{3,2,1,0:T(1,128)} %param.25) | copy-start | bytes 18436
  54.9 3.8 %collective-permute-start = (f32[8,512]{1,0:T(8,128)S(1)}, f32[8,512]{1,0:T(8,128)S(1)}, u32[]{:S(2)}, u32[]{:S(2)}) collective-permute-start(f32[8,512]{1,0:T(8,128)S(1)} %pad_maximum_fusion.3), channel_id=1, source_target_pairs={{0,2},{2,0},{1,3},{3,1},{4,6},{6,4},{5,7},{7,5},{8,10},{10,8},{9,1... | collective-permute-start | bytes 49160 | tf_op jit(solution)/shard_map/ppermute | solution.py:294
  58.7 5.8 %collective-permute-start.1 = (f32[8,1024]{1,0:T(8,128)S(1)}, f32[8,1024]{1,0:T(8,128)S(1)}, u32[]{:S(2)}, u32[]{:S(2)}) collective-permute-start(f32[8,1024]{1,0:T(8,128)S(1)} %pad_maximum_fusion.1), channel_id=1, source_target_pairs={{0,4},{4,8},{8,12},{12,0},{1,5},{5,9},{9,13},{13,1},{2,6},{6,10},{... | collective-permute-start | bytes 98312 | tf_op jit(solution)/shard_map/ppermute | solution.py:294
  58.8 5.7 %collective-permute-start.2 = (f32[8,1024]{1,0:T(8,128)S(1)}, f32[8,1024]{1,0:T(8,128)S(1)}, u32[]{:S(2)}, u32[]{:S(2)}) collective-permute-start(f32[8,1024]{1,0:T(8,128)S(1)} %pad_maximum_fusion.1), channel_id=1, source_target_pairs={{0,8},{4,12},{8,0},{12,4},{1,9},{5,13},{9,1},{13,5},{2,10},{6,14},... | collective-permute-start | bytes 98312 | tf_op jit(solution)/shard_map/ppermute | solution.py:294
  60.0 5.1 %collective-permute-start.3 = (f32[8,1024]{1,0:T(8,128)S(1)}, f32[8,1024]{1,0:T(8,128)S(1)}, u32[]{:S(2)}, u32[]{:S(2)}) collective-permute-start(f32[8,1024]{1,0:T(8,128)S(1)} %pad_maximum_fusion.1), channel_id=1, source_target_pairs={{0,12},{4,0},{8,4},{12,8},{1,13},{5,1},{9,5},{13,9},{2,14},{6,2},{... | collective-permute-start | bytes 98312 | tf_op jit(solution)/shard_map/ppermute | solution.py:294
  103.1 4.6 %collective-permute-start.4 = (f32[1,1024]{1,0:T(1,128)S(1)}, f32[1,1024]{1,0:T(1,128)S(1)}, u32[]{:S(2)}, u32[]{:S(2)}) collective-permute-start(f32[1,1024]{1,0:T(1,128)S(1)} %get-tuple-element.9), channel_id=1, source_target_pairs={{0,12},{4,0},{8,4},{12,8},{1,13},{5,1},{9,5},{13,9},{2,14},{6,2},{... | collective-permute-start | bytes 12296 | tf_op jit(solution)/shard_map/ppermute | solution.py:294
  106.3 4.5 %collective-permute-start.5 = (f32[1,1024]{1,0:T(1,128)S(1)}, f32[1,1024]{1,0:T(1,128)S(1)}, u32[]{:S(2)}, u32[]{:S(2)}) collective-permute-start(f32[1,1024]{1,0:T(1,128)S(1)} %get-tuple-element.11), channel_id=1, source_target_pairs={{0,8},{4,12},{8,0},{12,4},{1,9},{5,13},{9,1},{13,5},{2,10},{6,14},... | collective-permute-start | bytes 12296 | tf_op jit(solution)/shard_map/ppermute | solution.py:294
  106.6 5.4 %collective-permute-start.6 = (f32[1,1024]{1,0:T(1,128)S(1)}, f32[1,1024]{1,0:T(1,128)S(1)}, u32[]{:S(2)}, u32[]{:S(2)}) collective-permute-start(f32[1,1024]{1,0:T(1,128)S(1)} %get-tuple-element.10), channel_id=1, source_target_pairs={{0,4},{4,8},{8,12},{12,0},{1,5},{5,9},{9,13},{13,1},{2,6},{6,10},{... | collective-permute-start | bytes 12296 | tf_op jit(solution)/shard_map/ppermute | solution.py:294
  112.7 3.7 %collective-permute-start.7 = (f32[1,512]{1,0:T(1,128)S(1)}, f32[1,512]{1,0:T(1,128)S(1)}, u32[]{:S(2)}, u32[]{:S(2)}) collective-permute-start(f32[1,512]{1,0:T(1,128)S(1)} %slice.52), channel_id=1, source_target_pairs={{0,2},{2,0},{1,3},{3,1},{4,6},{6,4},{5,7},{7,5},{8,10},{10,8},{9,1... | collective-permute-start | bytes 6152 | tf_op jit(solution)/shard_map/ppermute | solution.py:294
  116.3 1.2 %collective-permute-start.8 = (f32[1,256]{1,0:T(1,128)S(1)}, f32[1,256]{1,0:T(1,128)S(1)}, u32[]{:S(2)}, u32[]{:S(2)}) collective-permute-start(f32[1,256]{1,0:T(1,128)S(1)} %constant_dynamic-slice_fusion), channel_id=1, source_target_pairs={{0,1},{1,0},{2,3},{3,2},{4,5},{5,4},{6,7},{7,6},{8,9},{9,8},{10,11... | collective-permute-start | bytes 3080 | tf_op jit(solution)/shard_map/ppermute | solution.py:294
where the time goes:
time: 119 us; the launch traced here: 118 us
  Pallas kernels  80 us (67%)
  waiting for transfers between devices  11.8 us (10%)
  starting transfers between devices  8.94 us (8%)
  local copies, waits for them, and re-layouts  7.3 us (6%)
  other arithmetic  5.42 us (5%)
  blocking collectives  3.86 us (3%)
    pallas_call x1, Pallas kernels, on_device(): pl.pallas_call(functools.partial(dynamics_kernel, tile_count=tile_count,...  43.4 us
    pallas_call x1, Pallas kernels, on_device(): pl.pallas_call(functools.partial(mesh_kernel, planes=planes, chunk=chunk,...  36.7 us
    ppermute x9, waiting for transfers between devices, passed_along(): return lax.ppermute(value, axis, pairs)  11.8 us
    ppermute x9, starting transfers between devices, passed_along(): return lax.ppermute(value, axis, pairs)  8.94 us
    unnamed x17, local copies, waits for them, and re-layouts  3.27 us
  transfers between devices with their start and end apart: 9, of which 7 were waited for; matrix products, arithmetic and copies ran while one was open for 3% of the time, Pallas kernels for 0%

commit v1 on v0

v1 whole, which is shorter than its diff:
```python
import functools
import math

import jax
import jax.numpy as jnp
import numpy as np
from jax import lax
from jax.experimental import pallas as pl
from jax.experimental.pallas import tpu as pltpu
from jax.sharding import PartitionSpec as P

GRID = 256
INNER = 4
LANES = 128
LOW = 128

time_step = 0.1
coulomb = 30.0
bond_stiffness = 0.2
soften = 1.0
cutoff_sq = 144.0
ewald_beta = 0.32

f32 = jnp.float32
bf16 = jnp.bfloat16


def lane_gather(rows, low):
    return jnp.take_along_axis(rows, low, axis=1, mode="promise_in_bounds")


def split(value):
    high = value.astype(bf16)
    return high, (value - high.astype(f32)).astype(bf16)


def single(left, right, turned=False):
    dims = (((1,), (1 if turned else 0,)), ((), ()))
    return lax.dot_general(left, right, dims, preferred_element_type=f32)


def product(left, right, turned=False):
    return single(left[0], right[0], turned) + (
        single(left[0], right[1], turned) + single(left[1], right[0], turned)
    )


def half_product(left, right, turned=False):
    return single(left[0], right, turned) + single(left[1], right, turned)


def spline(place, frac):
    rest = 1.0 - frac
    square = frac * frac
    cube = square * frac
    pieces = (
        rest * rest * rest / 6.0,
        (3.0 * cube - 6.0 * square + 4.0) / 6.0,
        (-3.0 * cube + 3.0 * square + 3.0 * frac + 1.0) / 6.0,
        cube / 6.0,
    )
    total = jnp.zeros(place.shape, f32)
    for order in range(4):
        total = jnp.where(place == order, pieces[order], total)
    return total


def wide_row(row):
    return jnp.broadcast_to(row, (8, LANES))


def stacked(rows):
    place = lax.broadcasted_iota(jnp.int32, (8, LANES), 0)
    total = jnp.zeros((8, LANES), rows[0].dtype)
    for r, row in enumerate(rows):
        total = jnp.where(place == r, wide_row(row), total)
    return total


def program_kernel(
    lines_ref, squares_ref,
    pos_hbm, vel_hbm, chg_hbm, imass_hbm, shown_hbm, parts_hbm, bonds_hbm, rest_hbm, offs_hbm,
    mine_hbm, cas_hbm, wide_hbm, tall_hbm, along_hbm, across_hbm,
    pos_out, vel_out, pot_out,
    pos_in, vel_in, chg_in, imass_in, shown_in, parts_in, bonds_in, rest_in, offs_in,
    mine_ref, cas_ref, wide_ref, tall_ref, along_ref, across_ref,
    parts_all, bonds_all, rest_all,
    mine, sent, beside, half_sent, half_recv, static_all, pos_all, vel_sent, vel_far,
    low_ref, blk_ref, shx_ref, shy_ref, qq_ref, near_ref, bforce, bidx_ref, brest_ref,
    grid, wx, wy, wyq, wz, part_sent, part_recv, pos_fin, vel_fin, pot_fin,
    load_sem, out_sem, step_send, step_recv, half_send_sem, half_recv_sem,
    pair_send, pair_recv, static_send, static_recv, place_send, place_recv, part_send_sem, part_recv_sem,
    *, tiles, pens, subs, planes, deep, share, lows, chunk, keep,
):
    ti, pi, si = lax.axis_index("tile"), lax.axis_index("pen"), lax.axis_index("sub")
    local = pens * subs
    group = tiles * local
    me = (ti * pens + pi) * subs + si
    atoms = pos_in.shape[3]
    width = atoms // subs
    chunks = width // LANES
    own_blocks = atoms // LANES
    slots = parts_all.shape[1]
    groups = subs * slots // 8
    bond_rows = bonds_all.shape[1]

    offsets = []
    for i in range(3):
        for j in range(3):
            step = ((i - 1) % tiles, (j - 1) % pens)
            if step != (0, 0) and step not in offsets:
                offsets.append(step)

    def remote(src, dst, send, recv, device):
        return pltpu.make_async_remote_copy(
            src_ref=src, dst_ref=dst, send_sem=send, recv_sem=recv,
            device_id=device, device_id_type=pl.DeviceIdType.MESH,
        )

    def tile_at(s):
        if tiles & (tiles - 1):
            return lax.rem(ti + s, tiles)
        total, bit = 0, 1
        while bit < tiles:
            total = total + lax.rem(lax.rem(lax.div(ti, bit), 2) + lax.rem(lax.div(s, bit), 2), 2) * bit
            bit *= 2
        return total

    def peer(d):
        s, rest = lax.div(d, local), lax.rem(d, local)
        t = tile_at(s)
        p = lax.rem(pi + lax.div(rest, subs), pens)
        q = lax.rem(si + lax.rem(rest, subs), subs)
        return {"tile": t, "pen": p, "sub": q}, (t * pens + p) * subs + q

    def each_peer(body):
        def step(d, carry):
            body(d, *peer(d))
            return carry

        lax.fori_loop(1, group, step, 0)

    half_lanes = pl.ds(pl.multiple_of(si * width, LANES), width)
    first_loads = [
        (parts_hbm.at[0, 0, :, half_lanes], parts_all.at[si]),
        (bonds_hbm.at[0, 0, :, half_lanes], bonds_all.at[si]),
        (rest_hbm.at[0, 0, :, half_lanes], rest_all.at[si]),
        (parts_hbm, parts_in), (bonds_hbm, bonds_in), (rest_hbm, rest_in),
        (pos_hbm, pos_in), (vel_hbm, vel_in), (chg_hbm, chg_in), (imass_hbm, imass_in),
        (shown_hbm, shown_in), (offs_hbm, offs_in),
    ]
    later_loads = [
        (mine_hbm.at[:, me], mine_ref), (cas_hbm, cas_ref), (wide_hbm, wide_ref), (tall_hbm, tall_ref),
        (along_hbm, along_ref), (across_hbm, across_ref),
    ]
    loads = [
        pltpu.make_async_copy(src, dst, load_sem.at[k]) for k, (src, dst) in enumerate(first_loads + later_loads)
    ]
    for copy in loads:
        copy.start()

    barrier = pltpu.get_barrier_semaphore()

    def greet(d, device, g):
        pl.semaphore_signal(barrier, inc=1, device_id=device, device_id_type=pl.DeviceIdType.MESH)

    each_peer(greet)
    for copy in loads[: len(first_loads)]:
        copy.wait()

    for c in range(chunks):
        lanes = pl.ds(pl.multiple_of(si * width + c * LANES, LANES), LANES)
        rows = [pos_in[r, 0, :, lanes] for r in range(3)] + [chg_in[0, :, lanes]]
        rows += [vel_in[r, 0, :, lanes] for r in range(3)] + [imass_in[0, :, lanes]]
        mine[c] = stacked(rows)
        offset = stacked([offs_in[r, 0, :, lanes].astype(f32) for r in range(3)])
        static_all[me, :, c * LANES : (c + 1) * LANES] = offset[:4]
    for step in range(1, subs):
        other = lax.rem(si + step, subs)
        for c in range(chunks):
            lanes = pl.ds(pl.multiple_of(other * width + c * LANES, LANES), LANES)
            half_recv[0, other, c] = stacked([pos_in[r, 0, :, lanes] for r in range(3)] + [chg_in[0, :, lanes]])[:4]

    shown = jnp.broadcast_to(shown_in[0], (8, LANES))
    shown_low, shown_high = shown & (LANES - 1), shown >> 7

    def step_copy(n, slot, q):
        dt, dp = offsets[slot]
        back = offsets.index(((-dt) % tiles, (-dp) % pens))
        device = {"tile": lax.rem(ti + dt, tiles), "pen": lax.rem(pi + dp, pens), "sub": q}
        return remote(sent.at[n], beside.at[n, back, si], step_send.at[n, slot, q], step_recv.at[n, back, si], device)

    def half_copy(n, step):
        other = lax.rem(si + step, subs)
        return remote(
            half_sent.at[n], half_recv.at[n, si], half_send_sem.at[n, step], half_recv_sem.at[n, si], {"sub": other}
        )

    def show(n):
        total = jnp.zeros((8, LANES), f32)
        for c in range(chunks):
            total = jnp.where(shown_high == si * chunks + c, lane_gather(mine[c], shown_low), total)
        sent[n] = total[:4]

    def send_shown(n):
        for slot in reversed(range(len(offsets))):
            for q in range(subs):
                step_copy(n, slot, q).start()

    def wait_shown(n):
        for slot in range(len(offsets)):
            for q in range(subs):
                remote(
                    sent.at[n], beside.at[n, slot, q], step_send.at[n, slot, q], step_recv.at[n, slot, q], {"sub": si}
                ).wait_recv()
                step_copy(n, slot, q).wait_send()

    show(0)
    pl.semaphore_wait(barrier, group - 1)
    send_shown(0)
    pairs = []
    for step in range(1, subs):
        other = lax.rem(si + step, subs)
        lanes = pl.ds(pl.multiple_of(other * width, LANES), width)
        for k, (source, target) in enumerate(
            ((parts_in, parts_all), (bonds_in, bonds_all), (rest_in, rest_all))
        ):
            pairs.append((k, step, source.at[0, 0, :, lanes], target, other))
    for k, step, source, target, other in pairs:
        remote(source, target.at[si], pair_send.at[k, step], pair_recv.at[k, si], {"sub": other}).start()

    def static_copy(d, device):
        return remote(static_all.at[me], static_all.at[me], static_send.at[d], static_recv.at[me], device)

    each_peer(lambda d, device, g: static_copy(d, device).start())
    for k, step, source, target, other in pairs:
        remote(source, target.at[other], pair_send.at[k, step], pair_recv.at[k, other], {"sub": other}).wait_recv()
        remote(source, target.at[si], pair_send.at[k, step], pair_recv.at[k, si], {"sub": other}).wait_send()

    moves_x, moves_y = [], []
    for i in range(3):
        near = ti + (i - 1)
        moves_x.append(jnp.where(near < 0, -float(GRID), jnp.where(near >= tiles, float(GRID), 0.0)))
        near = pi + (i - 1)
        moves_y.append(jnp.where(near < 0, -float(GRID), jnp.where(near >= pens, float(GRID), 0.0)))
    for c in range(chunks):
        for g in range(groups):
            q, row = divmod(g * 8, slots)
            index = parts_all[q, row : row + 8, c * LANES : (c + 1) * LANES]
            high = index >> 7
            block = high
            shx = jnp.zeros((8, LANES), f32)
            shy = jnp.zeros((8, LANES), f32)
            for i in range(3):
                for j in range(3):
                    if (i, j) == (1, 1):
                        continue
                    hit = high == own_blocks + i * 3 + j
                    step = ((i - 1) % tiles, (j - 1) % pens)
                    block = jnp.where(hit, own_blocks + offsets.index(step), block)
                    if i != 1:
                        shx = jnp.where(hit, moves_x[i], shx)
                    if j != 1:
                        shy = jnp.where(hit, moves_y[j], shy)
            low_ref[c, g] = index & (LANES - 1)
            blk_ref[c, g] = block
            shx_ref[c, g] = shx
            shy_ref[c, g] = shy
        atom = lax.broadcasted_iota(jnp.int32, (1, LANES), 1) + (si * width + c * LANES)
        every = [(q, b) for q in range(subs) for b in range(bond_rows)]
        for v in range(bidx_ref.shape[1]):
            part = every[v * 8 : v * 8 + 8]
            lanes = slice(c * LANES, (c + 1) * LANES)
            rows = [bonds_all[q, b : b + 1, lanes] for q, b in part]
            rows += [atom] * (8 - len(part))
            bidx_ref[c, v] = stacked(rows)
            brest_ref[c, v] = stacked([rest_all[q, b : b + 1, lanes] for q, b in part])

    def own_tables(rows):
        out = []
        for c in range(chunks):
            out.append((si * chunks + c, [wide_row(mine[c, r : r + 1, :]) for r in rows]))
        return out

    def far_tables(n, rows):
        out = []
        for step in range(1, subs):
            other = lax.rem(si + step, subs)
            for c in range(chunks):
                out.append((other * chunks + c, [wide_row(half_recv[n, other, c, r : r + 1, :]) for r in rows]))
        return out

    def around_tables(n, rows):
        out = []
        for slot in range(len(offsets)):
            patch = beside[n, slot, 0]
            for q in range(1, subs):
                patch = patch + beside[n, slot, q]
            out.append((own_blocks + slot, [wide_row(patch[r : r + 1, :]) for r in rows]))
        return out

    def pick(found, low, block, table):
        for number, sources in table:
            hit = block == number
            found = [jnp.where(hit, lane_gather(source, low), f) for source, f in zip(sources, found)]
        return found

    xyz = (0, 1, 2)

    def near_part(n, wait):
        table = own_tables(xyz)
        for c in range(chunks):
            for g in range(groups):
                found = pick([jnp.zeros((8, LANES), f32)] * 3, low_ref[c, g], blk_ref[c, g], table)
                for r in xyz:
                    near_ref[c, g, r] = found[r]
        if wait:
            for step in range(1, subs):
                other = lax.rem(si + step, subs)
                remote(
                    half_sent.at[n], half_recv.at[n, other], half_send_sem.at[n, step], half_recv_sem.at[n, other],
                    {"sub": other},
                ).wait_recv()
                half_copy(n, step).wait_send()
        more = far_tables(n, xyz)
        for c in range(chunks):
            for g in range(groups):
                found = [near_ref[c, g, r] for r in xyz]
                found = pick(found, low_ref[c, g], blk_ref[c, g], more)
                for r in xyz:
                    near_ref[c, g, r] = found[r]
            own = [wide_row(mine[c, r : r + 1, :]) for r in xyz]
            force = [jnp.zeros((8, LANES), f32)] * 3
            for v in range(bidx_ref.shape[1]):
                index = bidx_ref[c, v]
                near = pick([jnp.zeros((8, LANES), f32)] * 3, index & (LANES - 1), index >> 7, table + more)
                delta = [own[r] - near[r] for r in xyz]
                root = lax.rsqrt(delta[0] * delta[0] + delta[1] * delta[1] + delta[2] * delta[2] + soften)
                pull = -bond_stiffness * (1.0 - brest_ref[c, v] * root)
                force = [force[r] + pull * delta[r] for r in xyz]
            for r in xyz:
                bforce[c, r] = force[r]

    def far_part(n):
        table = around_tables(n, xyz)
        for c in range(chunks):
            own = [wide_row(mine[c, r : r + 1, :]) for r in xyz]
            force = [bforce[c, r] for r in xyz]
            for g in range(groups):
                near = pick([near_ref[c, g, r] for r in xyz], low_ref[c, g], blk_ref[c, g], table)
                delta = [own[0] - (near[0] + shx_ref[c, g]), own[1] - (near[1] + shy_ref[c, g]), own[2] - near[2]]
                dist_sq = delta[0] * delta[0] + delta[1] * delta[1] + delta[2] * delta[2]
                taper = 1.0 - dist_sq * (1.0 / cutoff_sq)
                taper = jnp.where(dist_sq < cutoff_sq, taper * taper, 0.0)
                root = lax.rsqrt(dist_sq + soften)
                strength = qq_ref[c, g] * taper * (root * root * root)
                force = [force[r] + strength * delta[r] for r in xyz]
            scale = mine[c, 7:8, :]
            for r in xyz:
                total = jnp.sum(force[r], axis=0, keepdims=True)
                speed = mine[c, 4 + r : 5 + r, :] + time_step * scale * total
                mine[c, 4 + r : 5 + r, :] = speed
                mine[c, r : r + 1, :] = mine[c, r : r + 1, :] + time_step * speed

    near_part(0, False)
    wait_shown(0)
    table = own_tables((3,)) + far_tables(0, (3,)) + around_tables(0, (3,))
    for c in range(chunks):
        own = wide_row(mine[c, 3:4, :])
        for g in range(groups):
            (near,) = pick([jnp.zeros((8, LANES), f32)], low_ref[c, g], blk_ref[c, g], table)
            qq_ref[c, g] = coulomb * own * near

    def inner(n, carry):
        far_part(n)
        for c in range(chunks):
            half_sent[n + 1, c] = mine[c][:4]
        show(n + 1)
        for step in range(1, subs):
            half_copy(n + 1, step).start()
        send_shown(n + 1)
        near_part(n + 1, True)
        wait_shown(n + 1)
        return carry

    lax.fori_loop(0, INNER - 1, inner, 0)
    far_part(INNER - 1)

    for c in range(chunks):
        lanes = slice(c * LANES, (c + 1) * LANES)
        pos_all[me, :, lanes] = mine[c][:4]
        vel_sent[:, lanes] = mine[c][4:]

    def place_copy(d, device):
        return remote(pos_all.at[me], pos_all.at[me], place_send.at[d], place_recv.at[me], device)

    def place_wait(g):
        remote(pos_all.at[me], pos_all.at[g], place_send.at[0], place_recv.at[g], {"sub": si}).wait_recv()

    def speed_copy(step):
        other = lax.rem(si + step, subs)
        return remote(vel_sent, vel_far.at[si], pair_send.at[3, step], pair_recv.at[3, si], {"sub": other})

    each_peer(lambda d, device, g: place_copy(d, device).start())
    for step in range(1, subs):
        speed_copy(step).start()

    for copy in loads[len(first_loads) :]:
        copy.wait()
    each_peer(
        lambda d, device, g: remote(
            static_all.at[me], static_all.at[g], static_send.at[d], static_recv.at[g], {"sub": si}
        ).wait_recv()
    )
    each_peer(lambda d, device, g: static_copy(d, device).wait_send())
    wide_atoms = local * width
    top = tiles * planes

    def cells(offset, count):
        return lax.broadcasted_iota(jnp.int32, (count, wide_atoms), 0) - offset

    def row_of(ref, t, r):
        return jnp.concatenate([ref[t * local + q, r : r + 1, :] for q in range(local)], axis=1)

    def prepare(t, r):
        offset = row_of(static_all, t, r)
        return offset.astype(jnp.int32), row_of(pos_all, t, r) - (offset + 1.0)

    def depth_of(t):
        offset, frac = prepare(t, 2)
        depth = spline(cells(offset, GRID) & (GRID - 1), frac)
        return split(product((cas_ref[0], cas_ref[1]), split(depth)))

    def clear(j, carry):
        for edge in range(tiles + 1):
            grid[j, edge * planes : edge * planes + 8] = jnp.zeros((8, GRID), f32)
        return carry

    lax.fori_loop(0, share, clear, 0)
    parts = [(c, min(c + chunk, lows), True) for c in range(0, lows, chunk)]
    parts += [(c, min(c + chunk, share), False) for c in range(lows, share, chunk)]

    def spread(s, carry):
        t = tile_at(s)

        def arrived(q, inner_carry):
            place_wait(t * local + lax.rem(pi * subs + si + q, local))
            return inner_carry

        @pl.when(s > 0)
        def _():
            place_wait(t * local + pi * subs + si)

        lax.fori_loop(1, local, arrived, 0)
        offset, frac = prepare(t, 0)
        wx[t] = spline(cells(offset - (t * planes - 1), deep), frac)
        offset, frac = prepare(t, 1)
        rows = spline(cells(offset, GRID) & (GRID - 1), frac)
        wy[t] = product((mine_ref[0], mine_ref[1]), split(rows))
        wyq[...] = wy[t] * row_of(pos_all, t, 3)
        depth = depth_of(t)
        if keep:
            wz[t, 0] = depth[0]
            wz[t, 1] = depth[1]
        base = pl.multiple_of(t * planes, 8)
        for start, stop, exact in parts:
            plane = jnp.concatenate([wx[t] * wyq[k : k + 1, :] for k in range(start, stop)], axis=0)
            if exact:
                values = product(split(plane), depth, True)
            else:
                values = half_product(split(plane), depth[0], True)
            values = values.reshape(stop - start, deep, GRID)
            for k in range(start, stop):
                value = values[k - start]
                grid[k, pl.ds(base, 8)] += value[:8]
                if planes > 8:
                    grid[k, pl.ds(pl.multiple_of(base + 8, 8), planes - 8)] = value[8:planes]
                grid[k, pl.ds(pl.multiple_of(base + planes, 8), 8)] += value[planes : planes + 8]
        return carry


    lax.fori_loop(0, tiles, spread, 0)
    for r in range(3):
        for q in range(subs):
            lanes = slice(q * width, (q + 1) * width)
            pos_fin[r, 0, :, lanes] = pos_all[(ti * pens + pi) * subs + q, r : r + 1, :]
    for r in range(3):
        for step in range(1, subs):
            other = lax.rem(si + step, subs)
            if r == 0:
                remote(
                    vel_sent, vel_far.at[other], pair_send.at[3, step], pair_recv.at[3, other], {"sub": other}
                ).wait_recv()
                speed_copy(step).wait_send()
            vel_fin[r, 0, :, pl.ds(pl.multiple_of(other * width, LANES), width)] = vel_far[other, r : r + 1, :]
        vel_fin[r, 0, :, half_lanes] = vel_sent[r : r + 1, :]
    outs = [
        pltpu.make_async_copy(pos_fin, pos_out, out_sem.at[0]),
        pltpu.make_async_copy(vel_fin, vel_out, out_sem.at[1]),
    ]
    for copy in outs:
        copy.start()

    def transform(exact):
        def step(k, carry):
            grid[k, 0:8] += grid[k, top : top + 8]
            line = grid[k, 0:top]
            spectrum = product((wide_ref[0], wide_ref[1]), split(line))
            m_sq = along_ref[...] + squares_ref[me * share + k]
            anchor = m_sq == 0.0
            value = across_ref[...] * lines_ref[me * share + k] / jnp.where(anchor, 1.0, m_sq)
            weighted = spectrum * jnp.where(anchor, 0.0, value)
            if exact:
                back = product((tall_ref[0], tall_ref[1]), split(weighted))
            else:
                back = half_product((tall_ref[0], tall_ref[1]), weighted.astype(bf16))
            grid[k, 0:top] = back
            grid[k, top : top + 8] = back[0:8]
            return carry

        return step

    lax.fori_loop(0, lows, transform(True), 0)
    lax.fori_loop(lows, share, transform(False), 0)

    def part_copy(g, device):
        return remote(part_sent.at[g], part_recv.at[me], part_send_sem.at[g], part_recv_sem.at[me], device)

    def device_of(g):
        return {"tile": lax.div(g, local), "pen": lax.rem(lax.div(g, subs), pens), "sub": lax.rem(g, subs)}

    def read(n, carry):
        s = tiles - 1 - n
        t = tile_at(s)
        if keep:
            depth = (wz[t, 0], wz[t, 1])
        else:
            depth = depth_of(t)
        base = pl.multiple_of(t * planes, 8)
        total = jnp.zeros((planes + 8, wide_atoms), f32)
        for start, stop, exact in parts:
            rows = [grid[k, pl.ds(base, planes + 8)] for k in range(start, stop)]
            line = jnp.concatenate(rows, axis=0)
            if exact:
                values = product(split(line), depth)
            else:
                values = half_product(split(line), depth[0])
            for k in range(start, stop):
                part = values[(k - start) * (planes + 8) : (k - start + 1) * (planes + 8)]
                total = total + part * wy[t, k : k + 1, :]
        result = jnp.sum(total * wx[t, : planes + 8], axis=0, keepdims=True)
        for q in range(local):
            part_sent[t * local + q] = result[:, q * width : (q + 1) * width]

        @pl.when(s > 0)
        def _():
            g = t * local + pi * subs + si
            part_copy(g, device_of(g)).start()

        def give(q, inner_carry):
            g = t * local + lax.rem(pi * subs + si + q, local)
            part_copy(g, device_of(g)).start()
            return inner_carry

        lax.fori_loop(1, local, give, 0)
        return carry

    lax.fori_loop(0, tiles, read, 0)
    part_recv[me] = part_sent[me]
    each_peer(lambda d, device, g: place_copy(d, device).wait_send())
    each_peer(lambda d, device, g: part_copy(g, device).wait_send())
    each_peer(
        lambda d, device, g: remote(
            part_sent.at[me], part_recv.at[g], part_send_sem.at[g], part_recv_sem.at[g], {"sub": si}
        ).wait_recv()
    )
    pot_fin[0] = jnp.sum(part_recv[...], axis=0)
    last = pltpu.make_async_copy(pot_fin, pot_out, out_sem.at[2])
    last.start()
    for copy in outs + [last]:
        copy.wait()


def halves(table):
    table = jnp.asarray(table.astype(np.float32))
    return jnp.stack(split(table))


def tables(group):
    share = GRID // group
    index = np.arange(GRID)
    angle = 2.0 * math.pi / GRID * np.mod(index[:, None] * index[None, :], GRID)
    cas = np.cos(angle) + np.sin(angle)
    wide = cas[:, np.mod(index - 1, GRID)]
    order = np.array([(r + 1) // 2 if r % 2 else (GRID - r // 2) % GRID for r in range(GRID)])
    dealt = order.reshape(share, group).T
    signed = np.where(index > GRID // 2, index - GRID, index).astype(np.float64)
    turn = 2.0 * math.pi / GRID * index
    real = (1.0 + 4.0 * np.cos(turn) + np.cos(2.0 * turn)) / 6.0
    imag = (4.0 * np.sin(turn) + np.sin(2.0 * turn)) / 6.0
    square = signed**2 / float(GRID * GRID)
    line = np.exp(-((math.pi / ewald_beta) ** 2) * square) / (real * real + imag * imag)
    along = square[:, None] + square[None, :]
    across = line[:, None] * line[None, :] / (math.pi * float(GRID) ** 3)
    flat = dealt.reshape(-1)
    return (
        cas, wide, cas[dealt], line[flat].astype(np.float32), square[flat].astype(np.float32),
        along.astype(np.float32), across.astype(np.float32),
    )


def on_device(
    positions, velocities, charges, inverse_mass, export_rows, partners, bond_partners, bond_rest, block_offsets,
):
    tiles, pens, subs = lax.axis_size("tile"), lax.axis_size("pen"), lax.axis_size("sub")
    local = pens * subs
    group = tiles * local
    atoms, exported = positions.shape[3], export_rows.shape[2]
    slots, bond_rows = partners.shape[2], bond_partners.shape[2]
    width = atoms // subs
    chunks = width // LANES
    groups = subs * slots // 8
    planes = GRID // tiles
    share = GRID // group
    lows = min(share, max(1, -(-LOW // group)))
    chunk = math.gcd(share, 4)
    unit = 8 if chunk % 2 == 0 else 16
    deep = -(-(planes + 8) // unit) * unit
    wide_atoms = local * width
    keep = group * width * GRID * 4 <= 16 * 1024 * 1024
    cas, wide, dealt, line, square, along, across = tables(group)
    around = {((i - 1) % tiles, (j - 1) % pens) for i in range(3) for j in range(3)} - {(0, 0)}
    near = len(around)
    bond_tiles = -(-subs * bond_rows // 8)
    assert exported == LANES and slots % 8 == 0 and planes % 8 == 0
    hbm = pl.BlockSpec(memory_space=pltpu.HBM)
    smem = pl.BlockSpec(memory_space=pltpu.SMEM)
    i32 = jnp.int32
    dma = pltpu.SemaphoreType.DMA

    def vmem(shape, kind=f32):
        return pltpu.VMEM(shape, kind)

    loaded = (
        positions, velocities, charges, inverse_mass, export_rows, partners, bond_partners, bond_rest, block_offsets,
    )
    constants = (halves(dealt), halves(cas), halves(wide), halves(wide.T), jnp.asarray(along), jnp.asarray(across))
    tile = (8, LANES)
    kernel = functools.partial(
        program_kernel, tiles=tiles, pens=pens, subs=subs, planes=planes, deep=deep, share=share, lows=lows,
        chunk=chunk, keep=keep,
    )
    return pl.pallas_call(
        kernel,
        out_shape=(
            jax.ShapeDtypeStruct(positions.shape, f32),
            jax.ShapeDtypeStruct(velocities.shape, f32),
            jax.ShapeDtypeStruct((1, 1, width), f32),
        ),
        in_specs=[smem] * 2 + [hbm] * (len(loaded) + len(constants)),
        out_specs=(hbm, hbm, hbm),
        scratch_shapes=[vmem(x.shape, x.dtype) for x in loaded]
        + [vmem((2, share, GRID), bf16)]
        + [vmem(x.shape, x.dtype) for x in constants[1:]]
        + [
            vmem((subs, slots, width), i32), vmem((subs, bond_rows, width), i32), vmem((subs, bond_rows, width)),
            vmem((chunks,) + tile), vmem((INNER, 4, LANES)), vmem((INNER, near, subs, 4, LANES)),
            vmem((INNER, chunks, 4, LANES)), vmem((INNER, subs, chunks, 4, LANES)),
            vmem((group, 4, width)), vmem((group, 4, width)), vmem((4, width)), vmem((subs, 4, width)),
            vmem((chunks, groups) + tile, i32), vmem((chunks, groups) + tile, i32),
            vmem((chunks, groups) + tile), vmem((chunks, groups) + tile), vmem((chunks, groups) + tile),
            vmem((chunks, groups, 3) + tile), vmem((chunks, 3) + tile),
            vmem((chunks, bond_tiles) + tile, i32), vmem((chunks, bond_tiles) + tile),
            vmem((share, GRID + 8, GRID)), vmem((tiles, deep, wide_atoms)), vmem((tiles, share, wide_atoms)),
            vmem((share, wide_atoms)), vmem((tiles if keep else 1, 2, GRID, wide_atoms), bf16),
            vmem((group, 1, width)), vmem((group, 1, width)),
            vmem(positions.shape), vmem(velocities.shape), vmem((1, 1, width)),
            dma((18,)), dma((3,)), dma((INNER, near, subs)), dma((INNER, near, subs)),
            dma((INNER, subs)), dma((INNER, subs)), dma((4, subs)), dma((4, subs)),
            dma((group,)), dma((group,)), dma((group,)), dma((group,)), dma((group,)), dma((group,)),
        ],
        compiler_params=pltpu.CompilerParams(
            collective_id=0, has_side_effects=True, vmem_limit_bytes=60 * 1024 * 1024
        ),
    )(jnp.asarray(line), jnp.asarray(square), *loaded, *constants)


def solution(mesh):
    placed = (
        P("rep", "tile", "pen", None),
        P("rep", "tile", "pen", None),
        P(("rep", "tile"), "pen", None),
        P(("rep", "tile"), "pen", None),
        P(("rep", "tile"), "pen", None),
        P(("rep", "tile"), "pen", "sub", None),
        P(("rep", "tile"), "pen", "sub", None),
        P(("rep", "tile"), "pen", "sub", None),
        P("rep", "tile", "pen", None),
    )
    return jax.shard_map(
        on_device,
        mesh=mesh,
        in_specs=placed,
        out_specs=(
            P("rep", "tile", "pen", None),
            P("rep", "tile", "pen", None),
            P(("rep", "tile"), "pen", "sub"),
        ),
        check_vma=False,
    )
```

time: 119 us -> 67.4 us (0.57)
  Pallas kernels: 80 us -> 64 us
  waiting for transfers between devices: 11.8 us -> 0 us
  starting transfers between devices: 8.94 us -> 0 us
  other arithmetic: 5.42 us -> 0 us
  local copies, waits for them, and re-layouts: 7.3 us -> 2.49 us
  blocking collectives: 3.86 us -> 0 us
    pallas_call x2 -> x1, Pallas kernels: 80 us -> 64 us  [on_device(): pl.pallas_call(kernel, out_shape=(jax.ShapeDtypeStruct(positions.shape, f...]
    ppermute x9 -> x0, waiting for transfers between devices: 11.8 us -> none  [passed_along(): return lax.ppermute(value, axis, pairs)]
    ppermute x9 -> x0, starting transfers between devices: 8.94 us -> none  [passed_along(): return lax.ppermute(value, axis, pairs)]
    all_gather x2 -> x0, blocking collectives: 3.86 us -> none  [the longest x1 2.05 us: on_device(): lax.all_gather(jnp.concatenate([partners[0, 0], bond_partners[0, 0]], axi...]
    another operation x3 -> x0, other arithmetic: 1.81 us -> none  [the longest x1 0.66 us: on_device(): jnp.stack([row] + [passed_along(row, 'tile', step) for step in range(1, t...]
    slice x4 -> x0, local copies, waits for them, and re-layouts: 1.39 us -> none  [the longest x1 0.72 us: on_device(): state[3:4]]
    dynamic_slice x2 -> x0, local copies, waits for them, and re-layouts: 1.32 us -> none  [the longest x1 1.32 us: on_device(): lax.dynamic_slice_in_dim(halves(cas), start, share, axis=1)]
    concatenate x4 -> x0, other arithmetic: 1.25 us -> none  [the longest x1 0.61 us: on_device(): jnp.concatenate([positions[:, 0, 0], charges[0], velocities[:, 0, 0], inv...]
  transfers between devices with their start and end apart: 9 -> 0, of which waited for: 7 -> 0; matrix products, arithmetic and copies ran while one was open for 3% -> 0% of each run, Pallas kernels for 0% -> 0%
where the time goes in v1:
time: 67.4 us; the launch traced here: 67.2 us
  Pallas kernels  64 us (95%)
  local copies, waits for them, and re-layouts  2.49 us (4%)
    pallas_call x1, Pallas kernels, on_device(): pl.pallas_call(kernel, out_shape=(jax.ShapeDtypeStruct(positions.shape, f...  64 us
    unnamed x7, local copies, waits for them, and re-layouts  2.49 us

profile of v1, /device:TPU:0, one launch (start us, length us, event | category | flops | bytes accessed | tf_op | source)
XLA Modules:
  0.0 67.2 jit_solution(14064753412353402842)
XLA Ops:
  0.6 64.0 %shard_map.184 = (f32[3,1,1,512]{3,2,1,0:T(1,128)}, f32[3,1,1,512]{3,2,1,0:T(1,128)}, f32[1,1,256]{2,1,0:T(1,128)}) custom-call(f32[256]{0:T(256)} %constant.22.clone.lines_ref, f32[256]{0:T(256)} %constant.23.clone.squares_ref, f32[3,1,1,512]{3,2,1,0:T(1,128)} %pos_hbm.1, f32[3,1,1,512]{3,2,1,0:T(1,128)} %vel_hbm.1, f32[1,1,512]{2,1,0:T(1,128)} %chg_hbm.1, ...), custom_call_target="tpu_custom_call" | custom-call | tf_op jit(solution)/shard_map/pallas_call | solution.py:653
  64.7 0.0 copy-start
  64.7 1.3 %copy.23 = f32[3,1,1,512]{3,2,1,0:T(1,128)} copy(f32[3,1,1,512]{3,2,1,0:T(1,128)} %get-tuple-element.6) | data formatting | bytes 12288
  66.0 0.0 copy-done
  66.0 0.0 copy-start.1
  66.0 0.6 copy.24
  66.6 0.0 copy-done.1
  66.6 0.6 copy.25
Async XLA Ops:
  64.7 1.3 %copy-start = (f32[3,1,1,512]{3,2,1,0:T(1,128)S(1)}, f32[3,1,1,512]{3,2,1,0:T(1,128)}, u32[]{:S(2)}) copy-start(f32[3,1,1,512]{3,2,1,0:T(1,128)} %get-tuple-element.7) | copy-start | bytes 18436
  66.0 0.6 copy-start.1

commit v2 on v1

--- a/solution.py
+++ b/solution.py
@@ -13,6 +13,7 @@
 INNER = 4
 LANES = 128
 LOW = 128
+BATCH = 4
 
 time_step = 0.1
 coulomb = 30.0
@@ -81,13 +82,13 @@
     lines_ref, squares_ref,
     pos_hbm, vel_hbm, chg_hbm, imass_hbm, shown_hbm, parts_hbm, bonds_hbm, rest_hbm, offs_hbm,
     mine_hbm, cas_hbm, wide_hbm, tall_hbm, along_hbm, across_hbm,
-    pos_out, vel_out, pot_out,
+    out_hbm,
     pos_in, vel_in, chg_in, imass_in, shown_in, parts_in, bonds_in, rest_in, offs_in,
     mine_ref, cas_ref, wide_ref, tall_ref, along_ref, across_ref,
     parts_all, bonds_all, rest_all,
     mine, sent, beside, half_sent, half_recv, static_all, pos_all, vel_sent, vel_far,
     low_ref, blk_ref, shx_ref, shy_ref, qq_ref, near_ref, bforce, bidx_ref, brest_ref,
-    grid, wx, wy, wyq, wz, part_sent, part_recv, pos_fin, vel_fin, pot_fin,
+    grid, wx, wy, wyq, wz, part_sent, part_recv, out_fin,
     load_sem, out_sem, step_send, step_recv, half_send_sem, half_recv_sem,
     pair_send, pair_recv, static_send, static_recv, place_send, place_recv, part_send_sem, part_recv_sem,
     *, tiles, pens, subs, planes, deep, share, lows, chunk, keep,
@@ -468,7 +469,7 @@
             if exact:
                 values = product(split(plane), depth, True)
             else:
-                values = half_product(split(plane), depth[0], True)
+                values = single(plane.astype(bf16), depth[0], True)
             values = values.reshape(stop - start, deep, GRID)
             for k in range(start, stop):
                 value = values[k - start]
@@ -483,45 +484,52 @@
     for r in range(3):
         for q in range(subs):
             lanes = slice(q * width, (q + 1) * width)
-            pos_fin[r, 0, :, lanes] = pos_all[(ti * pens + pi) * subs + q, r : r + 1, :]
+            out_fin[r, :, lanes] = pos_all[(ti * pens + pi) * subs + q, r : r + 1, :]
+    for step in range(1, subs):
+        other = lax.rem(si + step, subs)
+        remote(
+            vel_sent, vel_far.at[other], pair_send.at[3, step], pair_recv.at[3, other], {"sub": other}
+        ).wait_recv()
+        speed_copy(step).wait_send()
+        lanes = pl.ds(pl.multiple_of(other * width, LANES), width)
+        for r in range(3):
+            out_fin[3 + r, :, lanes] = vel_far[other, r : r + 1, :]
     for r in range(3):
-        for step in range(1, subs):
-            other = lax.rem(si + step, subs)
-            if r == 0:
-                remote(
-                    vel_sent, vel_far.at[other], pair_send.at[3, step], pair_recv.at[3, other], {"sub": other}
-                ).wait_recv()
-                speed_copy(step).wait_send()
-            vel_fin[r, 0, :, pl.ds(pl.multiple_of(other * width, LANES), width)] = vel_far[other, r : r + 1, :]
-        vel_fin[r, 0, :, half_lanes] = vel_sent[r : r + 1, :]
-    outs = [
-        pltpu.make_async_copy(pos_fin, pos_out, out_sem.at[0]),
-        pltpu.make_async_copy(vel_fin, vel_out, out_sem.at[1]),
-    ]
-    for copy in outs:
-        copy.start()
-
-    def transform(exact):
-        def step(k, carry):
-            grid[k, 0:8] += grid[k, top : top + 8]
-            line = grid[k, 0:top]
-            spectrum = product((wide_ref[0], wide_ref[1]), split(line))
-            m_sq = along_ref[...] + squares_ref[me * share + k]
-            anchor = m_sq == 0.0
-            value = across_ref[...] * lines_ref[me * share + k] / jnp.where(anchor, 1.0, m_sq)
-            weighted = spectrum * jnp.where(anchor, 0.0, value)
+        out_fin[3 + r, :, half_lanes] = vel_sent[r : r + 1, :]
+
+    def transform(start, stop, exact):
+        batch = math.gcd(math.gcd(start, stop), BATCH)
+
+        def step(n, carry):
+            first = start + n * batch
+            lines = []
+            for i in range(batch):
+                line = grid[first + i, 0:top]
+                edge = line[:8] + grid[first + i, top : top + 8]
+                lines.append(jnp.concatenate([edge, line[8:]], axis=0))
+            line = split(jnp.concatenate(lines, axis=1))
+            spectrum = product((wide_ref[0], wide_ref[1]), line)
+            weighted = []
+            for i in range(batch):
+                m_sq = along_ref[...] + squares_ref[me * share + first + i]
+                anchor = m_sq == 0.0
+                value = across_ref[...] * lines_ref[me * share + first + i] / jnp.where(anchor, 1.0, m_sq)
+                weighted.append(spectrum[:, i * GRID : (i + 1) * GRID] * jnp.where(anchor, 0.0, value))
+            weighted = jnp.concatenate(weighted, axis=1)
             if exact:
                 back = product((tall_ref[0], tall_ref[1]), split(weighted))
             else:
                 back = half_product((tall_ref[0], tall_ref[1]), weighted.astype(bf16))
-            grid[k, 0:top] = back
-            grid[k, top : top + 8] = back[0:8]
+            for i in range(batch):
+                grid[first + i, 0:top] = back[:, i * GRID : (i + 1) * GRID]
+                grid[first + i, top : top + 8] = back[0:8, i * GRID : (i + 1) * GRID]
             return carry
 
-        return step
-
-    lax.fori_loop(0, lows, transform(True), 0)
-    lax.fori_loop(lows, share, transform(False), 0)
+        if stop > start:
+            lax.fori_loop(0, (stop - start) // batch, step, 0)
+
+    transform(0, lows, True)
+    transform(lows, share, False)
 
     def part_copy(g, device):
         return remote(part_sent.at[g], part_recv.at[me], part_send_sem.at[g], part_recv_sem.at[me], device)
@@ -544,7 +552,7 @@
             if exact:
                 values = product(split(line), depth)
             else:
-                values = half_product(split(line), depth[0])
+                values = single(line.astype(bf16), depth[0])
             for k in range(start, stop):
                 part = values[(k - start) * (planes + 8) : (k - start + 1) * (planes + 8)]
                 total = total + part * wy[t, k : k + 1, :]
@@ -574,11 +582,11 @@
             part_sent.at[me], part_recv.at[g], part_send_sem.at[g], part_recv_sem.at[g], {"sub": si}
         ).wait_recv()
     )
-    pot_fin[0] = jnp.sum(part_recv[...], axis=0)
-    last = pltpu.make_async_copy(pot_fin, pot_out, out_sem.at[2])
+    out_fin[6, :, 0:width] = jnp.sum(part_recv[...], axis=0)
+    out_fin[6, :, width:] = jnp.zeros((1, atoms - width), f32)
+    last = pltpu.make_async_copy(out_fin, out_hbm, out_sem.at[0])
     last.start()
-    for copy in outs + [last]:
-        copy.wait()
+    last.wait()
 
 
 def halves(table):
@@ -650,15 +658,11 @@
         program_kernel, tiles=tiles, pens=pens, subs=subs, planes=planes, deep=deep, share=share, lows=lows,
         chunk=chunk, keep=keep,
     )
-    return pl.pallas_call(
+    out = pl.pallas_call(
         kernel,
-        out_shape=(
-            jax.ShapeDtypeStruct(positions.shape, f32),
-            jax.ShapeDtypeStruct(velocities.shape, f32),
-            jax.ShapeDtypeStruct((1, 1, width), f32),
-        ),
+        out_shape=jax.ShapeDtypeStruct((7, 1, atoms), f32),
         in_specs=[smem] * 2 + [hbm] * (len(loaded) + len(constants)),
-        out_specs=(hbm, hbm, hbm),
+        out_specs=hbm,
         scratch_shapes=[vmem(x.shape, x.dtype) for x in loaded]
         + [vmem((2, share, GRID), bf16)]
         + [vmem(x.shape, x.dtype) for x in constants[1:]]
@@ -674,7 +678,7 @@
             vmem((share, GRID + 8, GRID)), vmem((tiles, deep, wide_atoms)), vmem((tiles, share, wide_atoms)),
             vmem((share, wide_atoms)), vmem((tiles if keep else 1, 2, GRID, wide_atoms), bf16),
             vmem((group, 1, width)), vmem((group, 1, width)),
-            vmem(positions.shape), vmem(velocities.shape), vmem((1, 1, width)),
+            vmem((7, 1, atoms)),
             dma((18,)), dma((3,)), dma((INNER, near, subs)), dma((INNER, near, subs)),
             dma((INNER, subs)), dma((INNER, subs)), dma((4, subs)), dma((4, subs)),
             dma((group,)), dma((group,)), dma((group,)), dma((group,)), dma((group,)), dma((group,)),
@@ -683,6 +687,7 @@
             collective_id=0, has_side_effects=True, vmem_limit_bytes=60 * 1024 * 1024
         ),
     )(jnp.asarray(line), jnp.asarray(square), *loaded, *constants)
+    return out[0:3].reshape(positions.shape), out[3:6].reshape(velocities.shape), out[6:7, :, :width]
 
 
 def solution(mesh):

time: 67.4 us -> 59.4 us (0.88)
  Pallas kernels: 64 us -> 56 us
    pallas_call x1, Pallas kernels: 64 us -> 56 us  [on_device(): pl.pallas_call(kernel, out_shape=jax.ShapeDtypeStruct((7, 1, atoms), f32)...]
    slice x0 -> x1, local copies, waits for them, and re-layouts: none -> 1.2 us  [on_device(): out[6:7, :, :width]]
    unnamed x7 -> x1, local copies, waits for them, and re-layouts: 2.49 us -> 1.31 us
where the time goes in v2:
time: 59.4 us; the launch traced here: 59.2 us
  Pallas kernels  56 us (94%)
  local copies, waits for them, and re-layouts  2.51 us (4%)
  between operations  0.64 us (1%)
    pallas_call x1, Pallas kernels, on_device(): pl.pallas_call(kernel, out_shape=jax.ShapeDtypeStruct((7, 1, atoms), f32)...  56 us
    unnamed x1, local copies, waits for them, and re-layouts  1.31 us
    slice x1, local copies, waits for them, and re-layouts, on_device(): out[6:7, :, :width]  1.2 us

profile of v2, /device:TPU:0, one launch (start us, length us, event | category | flops | bytes accessed | tf_op | source)
XLA Modules:
  0.0 59.2 jit_solution(5801050216809736257)
XLA Ops:
  0.6 56.0 %shard_map.184 = f32[7,1,512]{2,1,0:T(1,128)} custom-call(f32[256]{0:T(256)} %constant.22.clone.lines_ref, f32[256]{0:T(256)} %constant.23.clone.squares_ref, f32[3,1,1,512]{3,2,1,0:T(1,128)} %pos_hbm.1, f32[3,1,1,512]{3,2,1,0:T(1,128)} %vel_hbm.1, f32[1,1,512]{2,1,0:T(1,128)} %chg_hbm.1, f32[1,1,512]{2,1,0:T(1,128)} %imass_hbm.1, s32[1,1,128]{2,1,0:T(1,128)} %shown_hbm.1, ...), custom_call_target="tpu_custom_call" | custom-call | tf_op jit(solution)/shard_map/pallas_call | solution.py:661
  56.7 1.3 %slice_bitcast_fusion = (f32[3,1,1,512]{3,2,1,0:T(1,128)}, f32[3,1,1,512]{3,2,1,0:T(1,128)}) fusion(f32[7,1,512]{2,1,0:T(1,128)} %shard_map.184), kind=kLoop, calls=%fused_computation | loop fusion | bytes 24576
  58.0 1.2 %slice.11 = f32[1,1,256]{2,1,0:T(1,128)} slice(f32[7,1,512]{2,1,0:T(1,128)} %shard_map.184), slice={[6:7], [0:1], [0:256]} | slice | bytes 2048 | tf_op jit(solution)/shard_map/slice | solution.py:690

commit v3 on v2

v3 whole, which is shorter than its diff:
```python
import functools
import math

import jax
import jax.numpy as jnp
import numpy as np
from jax import lax
from jax.experimental import pallas as pl
from jax.experimental.pallas import tpu as pltpu
from jax.sharding import PartitionSpec as P

GRID = 256
INNER = 4
LANES = 128
LOW = 128
BATCH = 8
VMEM_LIMIT = 60 * 1024 * 1024

time_step = 0.1
coulomb = 30.0
bond_stiffness = 0.2
soften = 1.0
cutoff_sq = 144.0
ewald_beta = 0.32

f32 = jnp.float32
bf16 = jnp.bfloat16


def lane_gather(rows, low):
    return jnp.take_along_axis(rows, low, axis=1, mode="promise_in_bounds")


def split(value):
    high = value.astype(bf16)
    return high, (value - high.astype(f32)).astype(bf16)


def single(left, right, turned=False):
    dims = (((1,), (1 if turned else 0,)), ((), ()))
    return lax.dot_general(left, right, dims, preferred_element_type=f32)


def product(left, right, turned=False):
    return single(left[0], right[0], turned) + (
        single(left[0], right[1], turned) + single(left[1], right[0], turned)
    )


def half_product(left, right, turned=False):
    return single(left[0], right, turned) + single(left[1], right, turned)


def spline_pieces(frac):
    rest = 1.0 - frac
    square = frac * frac
    cube = square * frac
    sixth = 1.0 / 6.0
    return (
        rest * rest * rest * sixth,
        (3.0 * cube - 6.0 * square + 4.0) * sixth,
        (-3.0 * cube + 3.0 * square + 3.0 * frac + 1.0) * sixth,
        cube * sixth,
    )


def spline(place, frac):
    pieces = spline_pieces(frac)
    total = jnp.zeros(place.shape, f32)
    for order in range(4):
        total = jnp.where(place == order, pieces[order], total)
    return total


def wide_row(row):
    return jnp.broadcast_to(row, (8, LANES))


def stacked(rows):
    place = lax.broadcasted_iota(jnp.int32, (8, LANES), 0)
    total = jnp.zeros((8, LANES), rows[0].dtype)
    for r, row in enumerate(rows):
        total = jnp.where(place == r, wide_row(row), total)
    return total


def program_kernel(
    pos_hbm, vel_hbm, chg_hbm, imass_hbm, shown_hbm, parts_hbm, bonds_hbm, rest_hbm, offs_hbm,
    mine_hbm, cas_hbm, tall_hbm, along_hbm, across_hbm, freq_hbm,
    out_ref,
    pos_in, vel_in, chg_in, imass_in, shown_in, parts_all, bonds_all, rest_all, offs_in,
    mine_ref, cas_ref, tall_ref, along_ref, across_ref, freq_ref,
    mine, sent, beside, static_all, pos_all, speeds,
    low_ref, blk_ref, shx_ref, shy_ref, qq_ref, near_ref, bforce, bidx_ref, brest_ref,
    grid, wx, wy, wyq, wz, gz, gy, part_sent, part_recv,
    load_sem, step_send, step_recv, pair_send, pair_recv,
    static_send, static_recv, place_send, place_recv, part_send_sem, part_recv_sem,
    *, tiles, pens, subs, planes, deep, share, lows, chunk, keep,
):
    ti, pi, si = lax.axis_index("tile"), lax.axis_index("pen"), lax.axis_index("sub")
    lead = subs - 1
    leads = si == lead
    local = pens * subs
    group = tiles * local
    patch = ti * pens + pi
    me = patch * subs + si
    atoms = pos_in.shape[3]
    width = atoms // subs
    chunks = atoms // LANES
    shown_chunk = chunks
    slots = parts_all.shape[1]
    groups = subs * slots // 8
    bond_rows = bonds_all.shape[1]
    everyone = range(chunks + 1)

    offsets = []
    for i in range(3):
        for j in range(3):
            step = ((i - 1) % tiles, (j - 1) % pens)
            if step != (0, 0) and step not in offsets:
                offsets.append(step)

    def remote(src, dst, send, recv, device):
        return pltpu.make_async_remote_copy(
            src_ref=src, dst_ref=dst, send_sem=send, recv_sem=recv,
            device_id=device, device_id_type=pl.DeviceIdType.MESH,
        )

    def shifted(index, step, count):
        if isinstance(step, int):
            moved = index + step % count
            return moved if step % count == 0 else jnp.where(moved >= count, moved - count, moved)
        return lax.rem(index + step, count)

    bits = []
    if tiles & (tiles - 1) == 0:
        bits = [lax.rem(lax.div(ti, 1 << b), 2) for b in range(tiles.bit_length() - 1)]

    def tile_at(s):
        if tiles & (tiles - 1):
            return shifted(ti, s, tiles)
        total = ti * 0
        for b, bit in enumerate(bits):
            if isinstance(s, int):
                total = total + ((1 - bit) if (s >> b) & 1 else bit) * (1 << b)
            else:
                total = total + lax.rem(bit + lax.rem(lax.div(s, 1 << b), 2), 2) * (1 << b)
        return total

    def peer(d):
        if isinstance(d, int):
            s, rest = divmod(d, local)
            p, q = divmod(rest, subs)
        else:
            s, rest = lax.div(d, local), lax.rem(d, local)
            p, q = lax.div(rest, subs), lax.rem(rest, subs)
        t, p, q = tile_at(s), shifted(pi, p, pens), shifted(si, q, subs)
        return {"tile": t, "pen": p, "sub": q}, (t * pens + p) * subs + q

    def each(first, last, body):
        if last - first <= 32:
            for d in range(first, last):
                body(d)
        else:
            def step(d, carry):
                body(d)
                return carry

            lax.fori_loop(first, last, step, 0)

    first_loads = [
        (parts_hbm.at[0, 0], parts_all.at[si]), (bonds_hbm.at[0, 0], bonds_all.at[si]),
        (rest_hbm.at[0, 0], rest_all.at[si]),
        (pos_hbm, pos_in), (vel_hbm, vel_in), (chg_hbm, chg_in), (imass_hbm, imass_in),
        (shown_hbm, shown_in), (offs_hbm, offs_in),
    ]
    later_loads = [
        (mine_hbm.at[:, me], mine_ref), (cas_hbm, cas_ref), (tall_hbm, tall_ref),
        (along_hbm, along_ref), (across_hbm, across_ref), (freq_hbm.at[me], freq_ref),
    ]
    loads = [
        pltpu.make_async_copy(src, dst, load_sem.at[k]) for k, (src, dst) in enumerate(first_loads + later_loads)
    ]
    for copy in loads[: len(first_loads)]:
        copy.start()

    barrier = pltpu.get_barrier_semaphore()
    each(
        1, group,
        lambda d: pl.semaphore_signal(
            barrier, inc=1, device_id=peer(d)[0], device_id_type=pl.DeviceIdType.MESH
        ),
    )
    for copy in loads[len(first_loads) :]:
        copy.start()
    for copy in loads[: len(first_loads)]:
        copy.wait()

    shown = jnp.broadcast_to(shown_in[0], (8, LANES))
    shown_low, shown_high = shown & (LANES - 1), shown >> 7

    def show(blocks):
        total = jnp.zeros((8, LANES), blocks[0].dtype)
        for c, block in enumerate(blocks):
            total = jnp.where(shown_high == c, lane_gather(block, shown_low), total)
        return total

    for c in range(chunks):
        lanes = slice(c * LANES, (c + 1) * LANES)
        rows = [pos_in[r, 0, :, lanes] for r in range(3)] + [chg_in[0, :, lanes]]
        rows += [vel_in[r, 0, :, lanes] for r in range(3)] + [imass_in[0, :, lanes]]
        mine[c] = stacked(rows)
        offset = stacked([offs_in[r, 0, :, lanes].astype(f32) for r in range(3)])
        static_all[patch, :, lanes] = offset[:4]
    mine[shown_chunk] = show([mine[c] for c in range(chunks)])

    def step_copy(n, slot):
        dt, dp = offsets[slot]
        back = offsets.index(((-dt) % tiles, (-dp) % pens))
        device = {"tile": shifted(ti, dt, tiles), "pen": shifted(pi, dp, pens)}
        return remote(sent.at[n], beside.at[n, back], step_send.at[n, slot], step_recv.at[n, back], device)

    def send_shown(n):
        sent[n] = mine[shown_chunk][:4]
        for slot in reversed(range(len(offsets))):
            step_copy(n, slot).start()

    def wait_shown(n):
        for slot in range(len(offsets)):
            remote(
                sent.at[n], beside.at[n, slot], step_send.at[n, slot], step_recv.at[n, slot], {"sub": si}
            ).wait_recv()
            step_copy(n, slot).wait_send()

    def pair_copy(k, source):
        table = (parts_all, bonds_all, rest_all, speeds)[k]
        if k == 3:
            return remote(speeds, speeds, pair_send.at[k, source], pair_recv.at[k, lead], {"sub": source})
        return remote(table.at[source], table.at[source], pair_send.at[k, source], pair_recv.at[k, source], {"sub": lead})

    def static_device(d):
        return {"tile": tile_at(d // pens if isinstance(d, int) else lax.div(d, pens)),
                "pen": shifted(pi, d % pens if isinstance(d, int) else lax.rem(d, pens), pens)}

    def static_copy(d):
        return remote(
            static_all.at[patch], static_all.at[patch], static_send.at[d], static_recv.at[patch], static_device(d)
        )

    pl.semaphore_wait(barrier, group - 1)

    @pl.when(leads)
    def _():
        send_shown(0)

    for source in range(lead):
        @pl.when(si == source)
        def _(source=source):
            for k in range(3):
                pair_copy(k, source).start()

    each(1, tiles * pens, lambda d: static_copy(d).start())

    moves_x, moves_y = [], []
    for i in range(3):
        near = ti + (i - 1)
        moves_x.append(jnp.where(near < 0, -float(GRID), jnp.where(near >= tiles, float(GRID), 0.0)))
        near = pi + (i - 1)
        moves_y.append(jnp.where(near < 0, -float(GRID), jnp.where(near >= pens, float(GRID), 0.0)))

    def work_out(c, g, index):
        high = index >> 7
        block = high
        shx = jnp.zeros((8, LANES), f32)
        shy = jnp.zeros((8, LANES), f32)
        for i in range(3):
            for j in range(3):
                if (i, j) == (1, 1):
                    continue
                hit = high == chunks + i * 3 + j
                step = ((i - 1) % tiles, (j - 1) % pens)
                block = jnp.where(hit, chunks + offsets.index(step), block)
                if i != 1:
                    shx = jnp.where(hit, moves_x[i], shx)
                if j != 1:
                    shy = jnp.where(hit, moves_y[j], shy)
        low_ref[c, g] = index & (LANES - 1)
        blk_ref[c, g] = block
        shx_ref[c, g] = shx
        shy_ref[c, g] = shy

    def set_up():
        for source in range(lead):
            for k in range(3):
                pair_copy(k, source).wait_recv()
        for g in range(groups):
            q, row = divmod(g * 8, slots)
            index = [parts_all[q, row : row + 8, c * LANES : (c + 1) * LANES] for c in range(chunks)]
            for c in everyone:
                work_out(c, g, show(index) if c == shown_chunk else index[c])
        rows_of = [(q, b) for q in range(subs) for b in range(bond_rows)]
        for v in range(bidx_ref.shape[1]):
            part = rows_of[v * 8 : v * 8 + 8]
            numbers, rests = [], []
            for c in range(chunks):
                lanes = slice(c * LANES, (c + 1) * LANES)
                atom = lax.broadcasted_iota(jnp.int32, (1, LANES), 1) + c * LANES
                rows = [bonds_all[q, b : b + 1, lanes] for q, b in part] + [atom] * (8 - len(part))
                numbers.append(stacked(rows))
                rests.append(stacked([rest_all[q, b : b + 1, lanes] for q, b in part]))
                bidx_ref[c, v] = numbers[c]
                brest_ref[c, v] = rests[c]
            bidx_ref[shown_chunk, v] = show(numbers)
            brest_ref[shown_chunk, v] = show(rests)

    def own_tables(rows):
        return [(c, [wide_row(mine[c, r : r + 1, :]) for r in rows]) for c in range(chunks)]

    def around_tables(n, rows):
        return [
            (chunks + slot, [wide_row(beside[n, slot, r : r + 1, :]) for r in rows]) for slot in range(len(offsets))
        ]

    def pick(found, low, block, table):
        for number, sources in table:
            hit = block == number
            found = [jnp.where(hit, lane_gather(source, low), f) for source, f in zip(sources, found)]
        return found

    xyz = (0, 1, 2)

    def near_part():
        table = own_tables(xyz)
        for c in everyone:
            for g in range(groups):
                found = pick([jnp.zeros((8, LANES), f32)] * 3, low_ref[c, g], blk_ref[c, g], table)
                near_ref[c, g, 0] = found[0] + shx_ref[c, g]
                near_ref[c, g, 1] = found[1] + shy_ref[c, g]
                near_ref[c, g, 2] = found[2]
            own = [wide_row(mine[c, r : r + 1, :]) for r in xyz]
            force = [jnp.zeros((8, LANES), f32)] * 3
            for v in range(bidx_ref.shape[1]):
                index = bidx_ref[c, v]
                near = pick([jnp.zeros((8, LANES), f32)] * 3, index & (LANES - 1), index >> 7, table)
                delta = [own[r] - near[r] for r in xyz]
                root = lax.rsqrt(delta[0] * delta[0] + delta[1] * delta[1] + delta[2] * delta[2] + soften)
                pull = -bond_stiffness * (1.0 - brest_ref[c, v] * root)
                force = [force[r] + pull * delta[r] for r in xyz]
            for r in xyz:
                bforce[c, r] = force[r]

    def far_part(n, which):
        table = around_tables(n, xyz)
        for c in which:
            own = [wide_row(mine[c, r : r + 1, :]) for r in xyz]
            force = [bforce[c, r] for r in xyz]
            for g in range(groups):
                shift = (shx_ref[c, g], shy_ref[c, g], 0.0)
                near = [near_ref[c, g, r] for r in xyz]
                low, block = low_ref[c, g], blk_ref[c, g]
                inside = block < chunks
                far = pick([jnp.zeros((8, LANES), f32)] * 3, low, block, table)
                near = [
                    jnp.where(inside, near[r], far[r] if r == 2 else far[r] + shift[r]) for r in xyz
                ]
                delta = [own[r] - near[r] for r in xyz]
                dist_sq = delta[0] * delta[0] + delta[1] * delta[1] + delta[2] * delta[2]
                taper = 1.0 - dist_sq * (1.0 / cutoff_sq)
                taper = jnp.where(dist_sq < cutoff_sq, taper * taper, 0.0)
                root = lax.rsqrt(dist_sq + soften)
                strength = qq_ref[c, g] * taper * (root * root * root)
                force = [force[r] + strength * delta[r] for r in xyz]
            scale = mine[c, 7:8, :]
            for r in xyz:
                total = jnp.sum(force[r], axis=0, keepdims=True)
                speed = mine[c, 4 + r : 5 + r, :] + time_step * scale * total
                mine[c, 4 + r : 5 + r, :] = speed
                mine[c, r : r + 1, :] = mine[c, r : r + 1, :] + time_step * speed

    def charges_once():
        table = own_tables((3,)) + around_tables(0, (3,))
        for c in everyone:
            own = wide_row(mine[c, 3:4, :])
            for g in range(groups):
                (near,) = pick([jnp.zeros((8, LANES), f32)], low_ref[c, g], blk_ref[c, g], table)
                qq_ref[c, g] = coulomb * own * near

    wide_atoms = local * width

    def cells(offset, count):
        return lax.broadcasted_iota(jnp.int32, (count, wide_atoms), 0) - offset

    def row_of(ref, t, r):
        return jnp.concatenate([ref[t * pens + p, r : r + 1, :] for p in range(pens)], axis=1)

    def static_wait(q):
        remote(
            static_all.at[patch], static_all.at[q], static_send.at[0], static_recv.at[q], {"sub": si}
        ).wait_recv()

    def place_wait(q):
        remote(
            pos_all.at[patch], pos_all.at[q], place_send.at[0], place_recv.at[q], {"sub": si}
        ).wait_recv()

    def tile_wait(wait, s, t, own_too):
        for step in range(1, pens):
            wait(t * pens + shifted(pi, step, pens))

        @pl.when(jnp.logical_or(s > 0, own_too))
        def _():
            wait(t * pens + pi)

    def fill(s):
        t = tile_at(s)
        tile_wait(static_wait, s, t, False)
        for r, source, target in ((1, mine_ref, gy), (2, cas_ref, gz)):
            offset = (row_of(static_all, t, r).astype(jnp.int32) + 1) & (GRID - 1)
            hot = jnp.where(cells(offset, GRID) == 0, 1.0, 0.0).astype(bf16)
            rows = source.shape[1]
            part = min(rows, GRID)
            for c in range(0, rows, part):
                value = single(source[0, c : c + part], hot) + single(source[1, c : c + part], hot)
                target[t, c : c + part] = value

    def fill_step(n):
        per = -(-tiles // INNER)
        for k in range(per):
            s = n * per + k
            if tiles % INNER:
                pl.when(s < tiles)(functools.partial(fill, s))
            else:
                fill(s)

    @pl.when(leads)
    def _():
        set_up()

    for copy in loads[len(first_loads) :]:
        copy.wait()

    def clear(j, carry):
        for edge in range(tiles + 1):
            grid[j, edge * planes : edge * planes + 8] = jnp.zeros((8, GRID), f32)
        return carry

    lax.fori_loop(0, share, clear, 0)

    def inner(n, carry):
        @pl.when(leads)
        def _():
            @pl.when(n > 0)
            def _():
                far_part(n - 1, [shown_chunk])
                send_shown(n)
                far_part(n - 1, range(chunks))

            near_part()

        if keep:
            fill_step(n)

        @pl.when(leads)
        def _():
            wait_shown(n)

            @pl.when(n == 0)
            def _():
                charges_once()

        return carry

    lax.fori_loop(0, INNER, inner, 0)

    def place_copy(d):
        return remote(pos_all.at[patch], pos_all.at[patch], place_send.at[d], place_recv.at[patch], peer(d)[0])

    @pl.when(leads)
    def _():
        far_part(INNER - 1, range(chunks))
        for c in range(chunks):
            lanes = slice(c * LANES, (c + 1) * LANES)
            pos_all[patch, :, lanes] = mine[c][:4]
            speeds[:, lanes] = mine[c][4:]
        each(1, group, lambda d: place_copy(d).start())
        for source in range(lead):
            pair_copy(3, source).start()

    if not keep:
        each(1, tiles * pens, lambda d: static_wait(
            static_device(d)["tile"] * pens + static_device(d)["pen"]
        ))
    each(1, tiles * pens, lambda d: static_copy(d).wait_send())
    top = tiles * planes

    def prepare(t, r):
        offset = row_of(static_all, t, r)
        return offset.astype(jnp.int32), row_of(pos_all, t, r) - (offset + 1.0)

    def blend(table, start, count, pieces):
        rows = table.shape[0] // 4
        total = table[start : start + count] * pieces[0]
        for m in range(1, 4):
            total = total + table[m * rows + start : m * rows + start + count] * pieces[m]
        return total

    def depth_of(t):
        offset, frac = prepare(t, 2)
        depth = spline(cells(offset, GRID) & (GRID - 1), frac)
        return split(product((cas_ref[0, GRID : 2 * GRID], cas_ref[1, GRID : 2 * GRID]), split(depth)))

    parts = [(c, min(c + chunk, lows), True) for c in range(0, lows, chunk)]
    parts += [(c, min(c + chunk, share), False) for c in range(lows, share, chunk)]

    def spread(s, carry):
        t = tile_at(s)
        tile_wait(place_wait, s, t, jnp.logical_not(leads))
        offset, frac = prepare(t, 0)
        wx[t] = spline(cells(offset - (t * planes - 1), deep), frac)
        offset, frac = prepare(t, 1)
        if keep:
            wy[t] = blend(gy.at[t], 0, share, spline_pieces(frac))
            pieces = spline_pieces(prepare(t, 2)[1])
            for c in range(0, GRID, 64):
                high, low = split(blend(gz.at[t], c, 64, pieces))
                wz[t, 0, c : c + 64] = high
                wz[t, 1, c : c + 64] = low
            depth = (wz[t, 0], wz[t, 1])
        else:
            rows = spline(cells(offset, GRID) & (GRID - 1), frac)
            wy[t] = product((mine_ref[0, share : 2 * share], mine_ref[1, share : 2 * share]), split(rows))
            depth = depth_of(t)
        wyq[...] = wy[t] * row_of(pos_all, t, 3)
        base = pl.multiple_of(t * planes, 8)
        for start, stop, exact in parts:
            plane = jnp.concatenate([wx[t] * wyq[k : k + 1, :] for k in range(start, stop)], axis=0)
            if exact:
                values = product(split(plane), depth, True)
            else:
                values = single(plane.astype(bf16), depth[0], True)
            values = values.reshape(stop - start, deep, GRID)
            for k in range(start, stop):
                value = values[k - start]
                grid[k, pl.ds(base, 8)] += value[:8]
                if planes > 8:
                    grid[k, pl.ds(pl.multiple_of(base + 8, 8), planes - 8)] = value[8:planes]
                grid[k, pl.ds(pl.multiple_of(base + planes, 8), 8)] += value[planes : planes + 8]
        return carry

    lax.fori_loop(0, tiles, spread, 0)
    for source in range(lead):
        @pl.when(si == source)
        def _(source=source):
            remote(
                speeds, speeds, pair_send.at[3, source], pair_recv.at[3, lead], {"sub": lead}
            ).wait_recv()
    for r in range(3):
        out_ref[r] = pos_all[patch, r : r + 1, :]
        out_ref[3 + r] = speeds[r : r + 1, :]

    def transform(start, stop, exact):
        batch = math.gcd(math.gcd(start, stop), BATCH)

        def step(n, carry):
            first = start + n * batch
            lines = []
            for i in range(batch):
                line = grid[first + i, 0:top]
                edge = line[:8] + grid[first + i, top : top + 8]
                lines.append(jnp.concatenate([edge, line[8:]], axis=0))
            line = split(jnp.concatenate(lines, axis=1))
            spectrum = product((cas_ref[0, :GRID], cas_ref[1, :GRID]), line)
            weighted = []
            for i in range(batch):
                m_sq = along_ref[...] + freq_ref[first + i, 0:1, :]
                anchor = m_sq == 0.0
                value = across_ref[...] * freq_ref[first + i, 1:2, :] / jnp.where(anchor, 1.0, m_sq)
                weighted.append(spectrum[:, i * GRID : (i + 1) * GRID] * jnp.where(anchor, 0.0, value))
            weighted = jnp.concatenate(weighted, axis=1)
            if exact:
                back = product((tall_ref[0], tall_ref[1]), split(weighted))
            else:
                back = half_product((tall_ref[0], tall_ref[1]), weighted.astype(bf16))
            for i in range(batch):
                grid[first + i, 0:top] = back[:, i * GRID : (i + 1) * GRID]
                grid[first + i, top : top + 8] = back[0:8, i * GRID : (i + 1) * GRID]
            return carry

        if stop > start:
            lax.fori_loop(0, (stop - start) // batch, step, 0)

    transform(0, lows, True)
    transform(lows, share, False)

    def part_copy(g, device):
        return remote(part_sent.at[g], part_recv.at[me], part_send_sem.at[g], part_recv_sem.at[me], device)

    def read(n, carry):
        s = tiles - 1 - n
        t = tile_at(s)
        if keep:
            depth = (wz[t, 0], wz[t, 1])
        else:
            depth = depth_of(t)
        base = pl.multiple_of(t * planes, 8)
        total = jnp.zeros((planes + 8, wide_atoms), f32)
        for start, stop, exact in parts:
            rows = [grid[k, pl.ds(base, planes + 8)] for k in range(start, stop)]
            line = jnp.concatenate(rows, axis=0)
            if exact:
                values = product(split(line), depth)
            else:
                values = single(line.astype(bf16), depth[0])
            for k in range(start, stop):
                part = values[(k - start) * (planes + 8) : (k - start + 1) * (planes + 8)]
                total = total + part * wy[t, k : k + 1, :]
        result = jnp.sum(total * wx[t, : planes + 8], axis=0, keepdims=True)
        for q in range(local):
            part_sent[t * local + q] = result[:, q * width : (q + 1) * width]

        def give(p, q):
            device = {"tile": t, "pen": p, "sub": q}
            part_copy((t * pens + p) * subs + q, device).start()

        for d in range(1, local):
            give(shifted(pi, d // subs, pens), shifted(si, d % subs, subs))

        @pl.when(s > 0)
        def _():
            give(pi, si)

        return carry

    lax.fori_loop(0, tiles, read, 0)
    part_recv[me] = part_sent[me]

    @pl.when(leads)
    def _():
        each(1, group, lambda d: place_copy(d).wait_send())
        for source in range(lead):
            pair_copy(3, source).wait_send()

    for source in range(lead):
        @pl.when(si == source)
        def _(source=source):
            for k in range(3):
                pair_copy(k, source).wait_send()

    def finish(d):
        device, g = peer(d)
        part_copy(g, device).wait_send()
        remote(part_sent.at[me], part_recv.at[g], part_send_sem.at[g], part_recv_sem.at[g], {"sub": si}).wait_recv()

    each(1, group, finish)
    out_ref[6, :, 0:width] = jnp.sum(part_recv[...], axis=0)
    out_ref[6, :, width:] = jnp.zeros((1, atoms - width), f32)


def halves(table):
    table = jnp.asarray(table.astype(np.float32))
    return jnp.stack(split(table))


def tables(group, shifts):
    share = GRID // group
    index = np.arange(GRID)
    angle = 2.0 * math.pi / GRID * np.mod(index[:, None] * index[None, :], GRID)
    cas = np.cos(angle) + np.sin(angle)
    order = np.array([(r + 1) // 2 if r % 2 else (GRID - r // 2) % GRID for r in range(GRID)])
    dealt = order.reshape(share, group).T
    signed = np.where(index > GRID // 2, index - GRID, index).astype(np.float64)
    turn = 2.0 * math.pi / GRID * index
    real = (1.0 + 4.0 * np.cos(turn) + np.cos(2.0 * turn)) / 6.0
    imag = (4.0 * np.sin(turn) + np.sin(2.0 * turn)) / 6.0
    square = signed**2 / float(GRID * GRID)
    line = np.exp(-((math.pi / ewald_beta) ** 2) * square) / (real * real + imag * imag)
    along = square[:, None] + square[None, :]
    across = line[:, None] * line[None, :] / (math.pi * float(GRID) ** 3)
    flat = dealt.reshape(-1)
    shifted = [cas[:, np.mod(index + m, GRID)] for m in range(-1, shifts - 1)]
    return (
        np.concatenate(shifted), shifted[0].T, np.concatenate([cells[dealt] for cells in shifted], axis=1), line[flat].astype(np.float32), square[flat].astype(np.float32),
        along.astype(np.float32), across.astype(np.float32),
    )


def on_device(
    positions, velocities, charges, inverse_mass, export_rows, partners, bond_partners, bond_rest, block_offsets,
):
    tiles, pens, subs = lax.axis_size("tile"), lax.axis_size("pen"), lax.axis_size("sub")
    local = pens * subs
    group = tiles * local
    atoms, exported = positions.shape[3], export_rows.shape[2]
    slots, bond_rows = partners.shape[2], bond_partners.shape[2]
    width = atoms // subs
    chunks = atoms // LANES
    groups = subs * slots // 8
    planes = GRID // tiles
    share = GRID // group
    lows = min(share, max(1, -(-LOW // group)))
    chunk = math.gcd(share, 8)
    unit = 8 if chunk % 2 == 0 else 16
    deep = -(-(planes + 8) // unit) * unit
    wide_atoms = local * width
    keep = group * width * GRID * 4 <= 16 * 1024 * 1024
    cas, tall, dealt, line, square, along, across = tables(group, 4 if keep else 2)
    around = {((i - 1) % tiles, (j - 1) % pens) for i in range(3) for j in range(3)} - {(0, 0)}
    near = len(around)
    bond_tiles = -(-subs * bond_rows // 8)
    assert exported == LANES and slots % 8 == 0 and planes % 8 == 0
    hbm = pl.BlockSpec(memory_space=pltpu.HBM)
    i32 = jnp.int32
    dma = pltpu.SemaphoreType.DMA

    def vmem(shape, kind=f32):
        return pltpu.VMEM(shape, kind)

    loaded = (
        positions, velocities, charges, inverse_mass, export_rows, partners, bond_partners, bond_rest, block_offsets,
    )
    freq = np.broadcast_to(np.stack([square, line], axis=1).reshape(group, share, 2, 1), (group, share, 2, GRID))
    constants = (
        halves(dealt), halves(cas), halves(tall), jnp.asarray(along), jnp.asarray(across), jnp.asarray(freq),
    )
    tile = (8, LANES)
    patches = tiles * pens
    scratch = [vmem(x.shape, x.dtype) for x in loaded]
    scratch[5:8] = [
        vmem((subs, slots, atoms), i32), vmem((subs, bond_rows, atoms), i32), vmem((subs, bond_rows, atoms)),
    ]
    kernel = functools.partial(
        program_kernel, tiles=tiles, pens=pens, subs=subs, planes=planes, deep=deep, share=share, lows=lows,
        chunk=chunk, keep=keep,
    )
    out = pl.pallas_call(
        kernel,
        out_shape=jax.ShapeDtypeStruct((7, 1, atoms), f32),
        in_specs=[hbm] * (len(loaded) + len(constants)),
        out_specs=pl.BlockSpec(memory_space=pltpu.VMEM),
        scratch_shapes=scratch
        + [vmem((2, dealt.shape[1], GRID), bf16)]
        + [vmem(x.shape, x.dtype) for x in constants[1:5]]
        + [
            vmem((share, 2, GRID)),
            vmem((chunks + 1,) + tile), vmem((INNER, 4, LANES)), vmem((INNER, near, 4, LANES)),
            vmem((patches, 4, atoms)), vmem((patches, 4, atoms)), vmem((4, atoms)),
            vmem((chunks + 1, groups) + tile, i32), vmem((chunks + 1, groups) + tile, i32),
            vmem((chunks + 1, groups) + tile), vmem((chunks + 1, groups) + tile), vmem((chunks + 1, groups) + tile),
            vmem((chunks + 1, groups, 3) + tile), vmem((chunks + 1, 3) + tile),
            vmem((chunks + 1, bond_tiles) + tile, i32), vmem((chunks + 1, bond_tiles) + tile),
            vmem((share, GRID + 8, GRID)), vmem((tiles, deep, wide_atoms)), vmem((tiles, share, wide_atoms)),
            vmem((share, wide_atoms)), vmem((tiles if keep else 1, 2, GRID, wide_atoms), bf16),
            vmem((tiles, 4 * GRID, wide_atoms) if keep else (1, 8, LANES)),
            vmem((tiles, 4 * share, wide_atoms) if keep else (1, 8, LANES)),
            vmem((group, 1, width)), vmem((group, 1, width)),
            dma((15,)), dma((INNER, near)), dma((INNER, near)), dma((4, subs)), dma((4, subs)),
            dma((patches,)), dma((patches,)), dma((group,)), dma((patches,)), dma((group,)), dma((group,)),
        ],
        compiler_params=pltpu.CompilerParams(
            collective_id=0, has_side_effects=True, vmem_limit_bytes=VMEM_LIMIT
        ),
    )(*loaded, *constants)
    return out[0:3].reshape(positions.shape), out[3:6].reshape(velocities.shape), out[6:7, :, :width]


def solution(mesh):
    placed = (
        P("rep", "tile", "pen", None),
        P("rep", "tile", "pen", None),
        P(("rep", "tile"), "pen", None),
        P(("rep", "tile"), "pen", None),
        P(("rep", "tile"), "pen", None),
        P(("rep", "tile"), "pen", "sub", None),
        P(("rep", "tile"), "pen", "sub", None),
        P(("rep", "tile"), "pen", "sub", None),
        P("rep", "tile", "pen", None),
    )
    return jax.shard_map(
        on_device,
        mesh=mesh,
        in_specs=placed,
        out_specs=(
            P("rep", "tile", "pen", None),
            P("rep", "tile", "pen", None),
            P(("rep", "tile"), "pen", "sub"),
        ),
        check_vma=False,
    )
```

time: 59.4 us -> 50.3 us (0.85)
  Pallas kernels: 56 us -> 44.9 us
  local copies, waits for them, and re-layouts: 2.51 us -> 4.57 us
    pallas_call x1, Pallas kernels: 56 us -> 44.9 us  [on_device(): pl.pallas_call(kernel, out_shape=jax.ShapeDtypeStruct((7, 1, atoms), f32)...]
    another operation x0 -> x1, local copies, waits for them, and re-layouts: none -> 2.03 us
where the time goes in v3:
time: 50.3 us; the launch traced here: 50.1 us
  Pallas kernels  44.9 us (89%)
  local copies, waits for them, and re-layouts  4.57 us (9%)
  between operations  0.64 us (1%)
    pallas_call x1, Pallas kernels, on_device(): pl.pallas_call(kernel, out_shape=jax.ShapeDtypeStruct((7, 1, atoms), f32)...  44.9 us
    another operation x1, local copies, waits for them, and re-layouts  2.03 us
    unnamed x1, local copies, waits for them, and re-layouts  1.31 us
    slice x1, local copies, waits for them, and re-layouts, on_device(): out[6:7, :, :width]  1.23 us

profile of v3, /device:TPU:0, one launch (start us, length us, event | category | flops | bytes accessed | tf_op | source)
XLA Modules:
  0.0 50.1 jit_solution(13481736482428131358)
XLA Ops:
  0.6 2.0 %jit_solution_.3.freq_hbm = f32[16,16,2,256]{3,2,1,0:T(2,128)} broadcast(f32[16,16,2]{2,1,0:T(8,128)} %constant.17.clone), dimensions={0,1,2} | broadcast | bytes 526336 | tf_op jit(solution)
  2.7 44.9 %shard_map.166 = f32[7,1,512]{2,1,0:T(1,128)} custom-call(f32[3,1,1,512]{3,2,1,0:T(1,128)} %pos_hbm.1, f32[3,1,1,512]{3,2,1,0:T(1,128)} %vel_hbm.1, f32[1,1,512]{2,1,0:T(1,128)} %chg_hbm.1, f32[1,1,512]{2,1,0:T(1,128)} %imass_hbm.1, s32[1,1,128]{2,1,0:T(1,128)} %shown_hbm.1, s32[1,1,32,512]{3,2,1,0:T(8,128)} %parts_hbm.1, s32[1,1,2,512]{3,2,1,0:T(2,128)} %bonds_hbm.1, ...), custom_call_target="tpu_custom_call" | custom-call | tf_op jit(solution)/shard_map/pallas_call | solution.py:735
  47.6 1.2 %slice.11 = f32[1,1,256]{2,1,0:T(1,128)} slice(f32[7,1,512]{2,1,0:T(1,128)} %shard_map.166), slice={[6:7], [0:1], [0:256]} | slice | bytes 2048 | tf_op jit(solution)/shard_map/slice | solution.py:763
  48.8 1.3 %slice_bitcast_fusion = (f32[3,1,1,512]{3,2,1,0:T(1,128)}, f32[3,1,1,512]{3,2,1,0:T(1,128)}) fusion(f32[7,1,512]{2,1,0:T(1,128)} %shard_map.166), kind=kLoop, calls=%fused_computation | loop fusion | bytes 24576

commit v4 on v3

--- a/solution.py
+++ b/solution.py
@@ -247,20 +247,6 @@
             static_all.at[patch], static_all.at[patch], static_send.at[d], static_recv.at[patch], static_device(d)
         )
 
-    pl.semaphore_wait(barrier, group - 1)
-
-    @pl.when(leads)
-    def _():
-        send_shown(0)
-
-    for source in range(lead):
-        @pl.when(si == source)
-        def _(source=source):
-            for k in range(3):
-                pair_copy(k, source).start()
-
-    each(1, tiles * pens, lambda d: static_copy(d).start())
-
     moves_x, moves_y = [], []
     for i in range(3):
         near = ti + (i - 1)
@@ -289,15 +275,20 @@
         shx_ref[c, g] = shx
         shy_ref[c, g] = shy
 
+    def set_up_rows(some):
+        for g in range(groups):
+            q, row = divmod(g * 8, slots)
+            if q not in some:
+                continue
+            index = [parts_all[q, row : row + 8, c * LANES : (c + 1) * LANES] for c in range(chunks)]
+            for c in everyone:
+                work_out(c, g, show(index) if c == shown_chunk else index[c])
+
     def set_up():
         for source in range(lead):
             for k in range(3):
                 pair_copy(k, source).wait_recv()
-        for g in range(groups):
-            q, row = divmod(g * 8, slots)
-            index = [parts_all[q, row : row + 8, c * LANES : (c + 1) * LANES] for c in range(chunks)]
-            for c in everyone:
-                work_out(c, g, show(index) if c == shown_chunk else index[c])
+        set_up_rows(range(lead))
         rows_of = [(q, b) for q in range(subs) for b in range(bond_rows)]
         for v in range(bidx_ref.shape[1]):
             part = rows_of[v * 8 : v * 8 + 8]
@@ -431,6 +422,21 @@
                 pl.when(s < tiles)(functools.partial(fill, s))
             else:
                 fill(s)
+
+    pl.when(leads)(functools.partial(set_up_rows, [lead]))
+    pl.semaphore_wait(barrier, group - 1)
+
+    @pl.when(leads)
+    def _():
+        send_shown(0)
+
+    for source in range(lead):
+        @pl.when(si == source)
+        def _(source=source):
+            for k in range(3):
+                pair_copy(k, source).start()
+
+    each(1, tiles * pens, lambda d: static_copy(d).start())
 
     @pl.when(leads)
     def _():
@@ -674,13 +680,15 @@
     imag = (4.0 * np.sin(turn) + np.sin(2.0 * turn)) / 6.0
     square = signed**2 / float(GRID * GRID)
     line = np.exp(-((math.pi / ewald_beta) ** 2) * square) / (real * real + imag * imag)
-    along = square[:, None] + square[None, :]
-    across = line[:, None] * line[None, :] / (math.pi * float(GRID) ** 3)
-    flat = dealt.reshape(-1)
+    along = square[:, None] + 0.5 * square[None, :]
+    across = line[:, None] * np.sqrt(line)[None, :] / (math.pi * float(GRID) ** 3)
+    freq = np.stack(
+        [square[dealt][..., None] + 0.5 * square, line[dealt][..., None] * np.sqrt(line)], axis=2
+    )
     shifted = [cas[:, np.mod(index + m, GRID)] for m in range(-1, shifts - 1)]
     return (
-        np.concatenate(shifted), shifted[0].T, np.concatenate([cells[dealt] for cells in shifted], axis=1), line[flat].astype(np.float32), square[flat].astype(np.float32),
-        along.astype(np.float32), across.astype(np.float32),
+        np.concatenate(shifted), shifted[0].T, np.concatenate([cells[dealt] for cells in shifted], axis=1),
+        freq.astype(np.float32), along.astype(np.float32), across.astype(np.float32),
     )
 
 
@@ -703,7 +711,7 @@
     deep = -(-(planes + 8) // unit) * unit
     wide_atoms = local * width
     keep = group * width * GRID * 4 <= 16 * 1024 * 1024
-    cas, tall, dealt, line, square, along, across = tables(group, 4 if keep else 2)
+    cas, tall, dealt, freq, along, across = tables(group, 4 if keep else 2)
     around = {((i - 1) % tiles, (j - 1) % pens) for i in range(3) for j in range(3)} - {(0, 0)}
     near = len(around)
     bond_tiles = -(-subs * bond_rows // 8)
@@ -718,7 +726,6 @@
     loaded = (
         positions, velocities, charges, inverse_mass, export_rows, partners, bond_partners, bond_rest, block_offsets,
     )
-    freq = np.broadcast_to(np.stack([square, line], axis=1).reshape(group, share, 2, 1), (group, share, 2, GRID))
     constants = (
         halves(dealt), halves(cas), halves(tall), jnp.asarray(along), jnp.asarray(across), jnp.asarray(freq),
     )

time: 50.3 us -> 48.4 us (0.962)
  local copies, waits for them, and re-layouts: 4.57 us -> 2.51 us
    another operation x1 -> x0, local copies, waits for them, and re-layouts: 2.03 us -> none
where the time goes in v4:
time: 48.4 us; the launch traced here: 48.1 us
  Pallas kernels  45 us (93%)
  local copies, waits for them, and re-layouts  2.51 us (5%)
  between operations  0.64 us (1%)
    pallas_call x1, Pallas kernels, on_device(): pl.pallas_call(kernel, out_shape=jax.ShapeDtypeStruct((7, 1, atoms), f32)...  45 us
    unnamed x1, local copies, waits for them, and re-layouts  1.31 us
    slice x1, local copies, waits for them, and re-layouts, on_device(): out[6:7, :, :width]  1.2 us

profile of v4, /device:TPU:0, one launch (start us, length us, event | category | flops | bytes accessed | tf_op | source)
XLA Modules:
  0.0 48.1 jit_solution(16569214637260471219)
XLA Ops:
  0.6 45.0 %shard_map.166 = f32[7,1,512]{2,1,0:T(1,128)} custom-call(f32[3,1,1,512]{3,2,1,0:T(1,128)} %pos_hbm.1, f32[3,1,1,512]{3,2,1,0:T(1,128)} %vel_hbm.1, f32[1,1,512]{2,1,0:T(1,128)} %chg_hbm.1, f32[1,1,512]{2,1,0:T(1,128)} %imass_hbm.1, s32[1,1,128]{2,1,0:T(1,128)} %shown_hbm.1, s32[1,1,32,512]{3,2,1,0:T(8,128)} %parts_hbm.1, s32[1,1,2,512]{3,2,1,0:T(2,128)} %bonds_hbm.1, ...), custom_call_target="tpu_custom_call" | custom-call | tf_op jit(solution)/shard_map/pallas_call | solution.py:742
  45.6 1.3 %slice_bitcast_fusion = (f32[3,1,1,512]{3,2,1,0:T(1,128)}, f32[3,1,1,512]{3,2,1,0:T(1,128)}) fusion(f32[7,1,512]{2,1,0:T(1,128)} %shard_map.166), kind=kLoop, calls=%fused_computation | loop fusion | bytes 24576
  46.9 1.2 %slice.11 = f32[1,1,256]{2,1,0:T(1,128)} slice(f32[7,1,512]{2,1,0:T(1,128)} %shard_map.166), slice={[6:7], [0:1], [0:256]} | slice | bytes 2048 | tf_op jit(solution)/shard_map/slice | solution.py:770

commit v5 on v4

--- a/solution.py
+++ b/solution.py
@@ -92,7 +92,7 @@
     mine_ref, cas_ref, tall_ref, along_ref, across_ref, freq_ref,
     mine, sent, beside, static_all, pos_all, speeds,
     low_ref, blk_ref, shx_ref, shy_ref, qq_ref, near_ref, bforce, bidx_ref, brest_ref,
-    grid, wx, wy, wyq, wz, gz, gy, part_sent, part_recv,
+    grid, wx, wy, wyq, wz, gz, gy, infl_ref, part_sent, part_recv,
     load_sem, step_send, step_recv, pair_send, pair_recv,
     static_send, static_recv, place_send, place_recv, part_send_sem, part_recv_sem,
     *, tiles, pens, subs, planes, deep, share, lows, chunk, keep,
@@ -175,8 +175,8 @@
         (shown_hbm, shown_in), (offs_hbm, offs_in),
     ]
     later_loads = [
+        (along_hbm, along_ref), (across_hbm, across_ref), (freq_hbm.at[me], freq_ref),
         (mine_hbm.at[:, me], mine_ref), (cas_hbm, cas_ref), (tall_hbm, tall_ref),
-        (along_hbm, along_ref), (across_hbm, across_ref), (freq_hbm.at[me], freq_ref),
     ]
     loads = [
         pltpu.make_async_copy(src, dst, load_sem.at[k]) for k, (src, dst) in enumerate(first_loads + later_loads)
@@ -424,6 +424,23 @@
                 fill(s)
 
     pl.when(leads)(functools.partial(set_up_rows, [lead]))
+    early = keep and share % INNER == 0
+
+    def influence(k):
+        m_sq = along_ref[...] + freq_ref[k, 0:1, :]
+        anchor = m_sq == 0.0
+        value = across_ref[...] * freq_ref[k, 1:2, :] / jnp.where(anchor, 1.0, m_sq)
+        return jnp.where(anchor, 0.0, value)
+
+    ready = loads[len(first_loads) : len(first_loads) + 3]
+    for copy in ready:
+        copy.wait()
+    if early:
+        def influence_row(k, carry):
+            infl_ref[k] = influence(k)
+            return carry
+
+        lax.fori_loop(0, share, influence_row, 0)
     pl.semaphore_wait(barrier, group - 1)
 
     @pl.when(leads)
@@ -442,7 +459,7 @@
     def _():
         set_up()
 
-    for copy in loads[len(first_loads) :]:
+    for copy in loads[len(first_loads) + 3 :]:
         copy.wait()
 
     def clear(j, carry):
@@ -578,10 +595,8 @@
             spectrum = product((cas_ref[0, :GRID], cas_ref[1, :GRID]), line)
             weighted = []
             for i in range(batch):
-                m_sq = along_ref[...] + freq_ref[first + i, 0:1, :]
-                anchor = m_sq == 0.0
-                value = across_ref[...] * freq_ref[first + i, 1:2, :] / jnp.where(anchor, 1.0, m_sq)
-                weighted.append(spectrum[:, i * GRID : (i + 1) * GRID] * jnp.where(anchor, 0.0, value))
+                value = infl_ref[first + i] if early else influence(first + i)
+                weighted.append(spectrum[:, i * GRID : (i + 1) * GRID] * value)
             weighted = jnp.concatenate(weighted, axis=1)
             if exact:
                 back = product((tall_ref[0], tall_ref[1]), split(weighted))
@@ -759,6 +774,7 @@
             vmem((share, wide_atoms)), vmem((tiles if keep else 1, 2, GRID, wide_atoms), bf16),
             vmem((tiles, 4 * GRID, wide_atoms) if keep else (1, 8, LANES)),
             vmem((tiles, 4 * share, wide_atoms) if keep else (1, 8, LANES)),
+            vmem((share, GRID, GRID) if keep and share % INNER == 0 else (1, 8, LANES)),
             vmem((group, 1, width)), vmem((group, 1, width)),
             dma((15,)), dma((INNER, near)), dma((INNER, near)), dma((4, subs)), dma((4, subs)),
             dma((patches,)), dma((patches,)), dma((group,)), dma((patches,)), dma((group,)), dma((group,)),

time: 48.4 us -> 47.8 us (0.988)
  Pallas kernels: 45 us -> 44.4 us
    pallas_call x1, Pallas kernels: 45 us -> 44.4 us  [on_device(): pl.pallas_call(kernel, out_shape=jax.ShapeDtypeStruct((7, 1, atoms), f32)...]
where the time goes in v5:
time: 47.8 us; the launch traced here: 47.5 us
  Pallas kernels  44.4 us (93%)
  local copies, waits for them, and re-layouts  2.51 us (5%)
  between operations  0.64 us (1%)
    pallas_call x1, Pallas kernels, on_device(): pl.pallas_call(kernel, out_shape=jax.ShapeDtypeStruct((7, 1, atoms), f32)...  44.4 us
    unnamed x1, local copies, waits for them, and re-layouts  1.31 us
    slice x1, local copies, waits for them, and re-layouts, on_device(): out[6:7, :, :width]  1.2 us

profile of v5, /device:TPU:0, one launch (start us, length us, event | category | flops | bytes accessed | tf_op | source)
XLA Modules:
  0.0 47.5 jit_solution(16864422983388894621)
XLA Ops:
  0.6 44.4 %shard_map.166 = f32[7,1,512]{2,1,0:T(1,128)} custom-call(f32[3,1,1,512]{3,2,1,0:T(1,128)} %pos_hbm.1, f32[3,1,1,512]{3,2,1,0:T(1,128)} %vel_hbm.1, f32[1,1,512]{2,1,0:T(1,128)} %chg_hbm.1, f32[1,1,512]{2,1,0:T(1,128)} %imass_hbm.1, s32[1,1,128]{2,1,0:T(1,128)} %shown_hbm.1, s32[1,1,32,512]{3,2,1,0:T(8,128)} %parts_hbm.1, s32[1,1,2,512]{3,2,1,0:T(2,128)} %bonds_hbm.1, ...), custom_call_target="tpu_custom_call" | custom-call | tf_op jit(solution)/shard_map/pallas_call | solution.py:757
  45.0 1.3 %slice_bitcast_fusion = (f32[3,1,1,512]{3,2,1,0:T(1,128)}, f32[3,1,1,512]{3,2,1,0:T(1,128)}) fusion(f32[7,1,512]{2,1,0:T(1,128)} %shard_map.166), kind=kLoop, calls=%fused_computation | loop fusion | bytes 24576
  46.3 1.2 %slice.11 = f32[1,1,256]{2,1,0:T(1,128)} slice(f32[7,1,512]{2,1,0:T(1,128)} %shard_map.166), slice={[6:7], [0:1], [0:256]} | slice | bytes 2048 | tf_op jit(solution)/shard_map/slice | solution.py:786
